TPU v7x, 32 devices: a whole 2x2x4 slice. The times are simulated.
32 devices in a mesh: rep: 8 (over z, core), shard: 4 (over y, x).
Axes of the slice: x: 2, y: 2, z: 4, core: 2. Of those that a mesh axis runs over, the one named last changes fastest.
Arguments:
- block_in: bfloat16 [4096, 2048], P(('rep', 'shard')), may hold values from -6 to 6
- segments: int32 [4096], P('rep'), may hold values from 0 to 15, never falling along the last dimension, each value on 1 to 512 neighbouring positions
- routes: int32 [4096, 8], P(('rep', 'shard')), may hold values from 0 to 31, all different within a row; in each aligned block of 128 rows (0 to 127, 128 to 255, ...) at most 64 rows name the same one
- attn_gain: float32 [2048], replicated, may hold values from 0.25 to 1.75
- query_key_value_weight: bfloat16 [2048, 5120], P('shard'), may hold values from -0.125 to 0.125
- q_gain: float32 [128], replicated, may hold values from 0.25 to 1.75
- k_gain: float32 [128], replicated, may hold values from 0.25 to 1.75
- w_out: bfloat16 [4096, 2048], P('shard'), may hold values from -1.5 to 1.5
- ffn_gain: float32 [2048], replicated, may hold values from 0.25 to 1.75
- router: bfloat16 [2048, 32], replicated, may hold values from -0.09375 to 0.09375
- expert_weights: bfloat16 [32, 3, 2048, 768], P(('rep', 'shard')), may hold values from -0.125 to 0.125
- cotangent: bfloat16 [4096, 2048], P(('rep', 'shard')), may hold values from -6 to 6
Outputs:
- block_out: bfloat16 [4096, 2048], P(('rep', 'shard'))
- grad_input: bfloat16 [4096, 2048], P(('rep', 'shard'))
- grad_attn_gain: float32 [2048], replicated
- grad_qkv: float32 [2048, 5120], P('shard')
- grad_q_gain: float32 [128], replicated
- grad_k_gain: float32 [128], replicated
- grad_out: float32 [4096, 2048], P('shard')
- grad_ffn_gain: float32 [2048], replicated
- grad_router: float32 [2048, 32], replicated
- grad_experts: float32 [32, 3, 2048, 768], P(('rep', 'shard'))
Inputs may be any that keep to these rules, and one draw needn't show every extreme that they name: `segments`: document numbers never fall along the tokens; a document has 1 to 512 tokens and one has exactly 512. `routes`: each row names 8 different experts; among the 128 rows of one device no expert is named more than 64 times, and in every draw some device names some expert exactly 64 times.
All inputs are finite; a program needn't handle non-finite values.
Results may differ from a plain program's by a relative error of at most 0.02.
Values may be sent and summed in bfloat16 or wider, within the bound.
A program may use at most 384 MiB of HBM per device.

v0:
```python
import functools

import jax
import jax.numpy as jnp
from jax import lax
from jax.experimental import pallas as pl
from jax.experimental.pallas import tpu as pltpu
from jax.sharding import PartitionSpec as P


QUERY_HEADS = 32
KEY_VALUE_HEADS = 4
HEAD_SIZE = 128


epsilon = 1e-06
rope_base = 1000000.0


def product(form, left, right):
    return jnp.einsum(form, left, right, preferred_element_type=jnp.float32)


def rms_scale(values):
    return lax.rsqrt(jnp.mean(values * values, axis=-1, keepdims=True) + epsilon)


def rms_back(values, scale, gain, upstream):
    scaled = upstream * gain
    cube = scale * scale * scale
    grad_values = scale * scaled - values * cube * jnp.mean(scaled * values, axis=-1, keepdims=True)
    grad_gain = jnp.sum((upstream * values * scale).reshape(-1, values.shape[-1]), axis=0)
    return (grad_values, grad_gain)


def rope_tables(positions):
    half = HEAD_SIZE // 2
    freq = rope_base ** (-jnp.arange(half).astype(jnp.float32) * 2.0 / HEAD_SIZE)
    angles = positions.astype(jnp.float32)[:, None] * freq[None, :]
    cosine = jnp.concatenate([jnp.cos(angles), jnp.cos(angles)], axis=-1)
    sine = jnp.concatenate([jnp.sin(angles), jnp.sin(angles)], axis=-1)
    return (cosine[:, None, :], sine[:, None, :])


def rotate(values):
    half = values.shape[-1] // 2
    return jnp.concatenate([-values[..., half:], values[..., :half]], axis=-1)


def rotate_back(values):
    half = values.shape[-1] // 2
    return jnp.concatenate([values[..., half:], -values[..., :half]], axis=-1)


def split_heads(query_key_value):
    token_rows = query_key_value.shape[0]
    q_raw = query_key_value[:, : QUERY_HEADS * HEAD_SIZE].reshape(
        token_rows, QUERY_HEADS, HEAD_SIZE
    )
    unrotated_key = query_key_value[
        :, QUERY_HEADS * HEAD_SIZE : (QUERY_HEADS + KEY_VALUE_HEADS) * HEAD_SIZE
    ].reshape(token_rows, KEY_VALUE_HEADS, HEAD_SIZE)
    projected_value = query_key_value[:, (QUERY_HEADS + KEY_VALUE_HEADS) * HEAD_SIZE :].reshape(
        token_rows, KEY_VALUE_HEADS, HEAD_SIZE
    )
    return (q_raw, unrotated_key, projected_value)


def norm_rope(raw, gain, cosine, sine):
    scale = rms_scale(raw)
    normed = raw * scale * gain
    return (scale, (normed * cosine + rotate(normed) * sine).astype(jnp.bfloat16))


def norm_rope_back(raw, scale, gain, cosine, sine, grad_rot):
    grad_normed = grad_rot * cosine + rotate_back(grad_rot * sine)
    return rms_back(raw, scale, gain, grad_normed)


def split_groups(values, groups):
    token_rows, heads, width = values.shape
    return values.reshape(token_rows, groups, heads // groups, width).transpose(1, 0, 2, 3)


def attend_forward(queries, keys, values, allowed):
    groups = keys.shape[1]
    token_rows = queries.shape[0]
    scale = queries.shape[2] ** (-0.5)

    def one_group(operands):
        q_part, k_part, v_part = operands
        scores = jnp.where(allowed[None], product("tpd,sd->pts", q_part, k_part) * scale, -1e30)
        highest = jnp.max(scores, axis=2, keepdims=True)
        lse = highest + jnp.log(jnp.sum(jnp.exp(scores - highest), axis=2, keepdims=True))
        probs = jnp.exp(scores - lse).astype(jnp.bfloat16)
        return (product("pts,sd->tpd", probs, v_part), lse[:, :, 0])

    outputs, lse = lax.map(
        one_group,
        (split_groups(queries, groups), keys.transpose(1, 0, 2), values.transpose(1, 0, 2)),
    )
    return (outputs.transpose(1, 0, 2, 3).reshape(token_rows, -1), lse)


def attend_backward(queries, keys, values, allowed, lse, attended, grad_attended):
    groups = keys.shape[1]
    token_rows, heads, width = queries.shape
    scale = width ** (-0.5)

    def one_group(operands):
        q_part, k_part, v_part, lse_part, out_part, grad_part = operands
        scores = jnp.where(allowed[None], product("tpd,sd->pts", q_part, k_part) * scale, -1e30)
        probs = jnp.exp(scores - lse_part[:, :, None])
        grad_v = product("pts,tpd->sd", probs.astype(jnp.bfloat16), grad_part)
        grad_p = product("tpd,sd->pts", grad_part, v_part)
        delta = jnp.sum(
            out_part.astype(jnp.float32) * grad_part.astype(jnp.float32), axis=2
        ).transpose(1, 0)
        grad_score = (probs * (grad_p - delta[:, :, None]) * scale).astype(jnp.bfloat16)
        return (
            product("pts,sd->tpd", grad_score, k_part),
            product("pts,tpd->sd", grad_score, q_part),
            grad_v,
        )

    shaped_out = split_groups(attended.reshape(token_rows, heads, width), groups)
    shaped_grad = split_groups(grad_attended.reshape(token_rows, heads, width), groups)
    grad_q, grad_k, grad_v = lax.map(
        one_group,
        (
            split_groups(queries, groups),
            keys.transpose(1, 0, 2),
            values.transpose(1, 0, 2),
            lse,
            shaped_out,
            shaped_grad,
        ),
    )
    return (
        grad_q.transpose(1, 0, 2, 3).reshape(token_rows, heads, width),
        grad_k.transpose(1, 0, 2),
        grad_v.transpose(1, 0, 2),
    )


def route_gates(normed, router, routes):
    logits = jnp.dot(normed, router, preferred_element_type=jnp.float32)
    weights = jax.nn.softmax(logits, axis=-1)
    chosen = (
        routes[:, :, None] == jnp.arange(router.shape[1], dtype=jnp.int32)[None, None, :]
    ).astype(jnp.float32)
    picked = jnp.sum(chosen * weights[:, None, :], axis=2)
    total = jnp.sum(picked, axis=1, keepdims=True)
    return (weights, chosen, picked, total, picked / total)


def route_gates_back(normed, router, weights, chosen, picked, total, grad_gates):
    grad_picked = grad_gates / total - jnp.sum(grad_gates * picked, axis=1, keepdims=True) / (
        total * total
    )
    grad_weights = jnp.sum(chosen * grad_picked[:, :, None], axis=1)
    grad_logits = weights * (grad_weights - jnp.sum(grad_weights * weights, axis=1, keepdims=True))
    grad_normed = jnp.dot(
        grad_logits, router.astype(jnp.float32).T, precision=lax.Precision.HIGHEST
    )
    grad_router = jnp.dot(
        normed.astype(jnp.float32).T, grad_logits, precision=lax.Precision.HIGHEST
    )
    return (grad_normed, grad_router)


def route_index(routes, experts, capacity):
    flat = routes.reshape(-1)
    onehot = (flat[:, None] == jnp.arange(experts, dtype=jnp.int32)[None, :]).astype(jnp.int32)
    before = jnp.cumsum(onehot, axis=0) - onehot
    return flat * capacity + jnp.sum(before * onehot, axis=1)


def dispatch(rows_per_route, index, experts, capacity):
    width = rows_per_route.shape[1]
    empty = jnp.zeros((experts * capacity, width), rows_per_route.dtype)
    return empty.at[index].set(rows_per_route).reshape(experts, capacity, width)


def collect(buffer, index):
    return buffer.reshape(-1, buffer.shape[-1])[index]


def expert_forward(inputs, weights):
    gate_pre = product("ecd,edf->ecf", inputs, weights[:, 0])
    up_pre = product("ecd,edf->ecf", inputs, weights[:, 1])
    hidden = (jax.nn.silu(gate_pre) * up_pre).astype(jnp.bfloat16)
    result = product("ecf,edf->ecd", hidden, weights[:, 2]).astype(jnp.bfloat16)
    return (gate_pre, up_pre, hidden, result)


def expert_backward(weights, gate_pre, up_pre, grad_result):
    grad_hidden = product("ecd,edf->ecf", grad_result, weights[:, 2])
    sig = jax.nn.sigmoid(gate_pre)
    grad_gate = (grad_hidden * up_pre * sig * (1.0 + gate_pre * (1.0 - sig))).astype(jnp.bfloat16)
    grad_up = (grad_hidden * gate_pre * sig).astype(jnp.bfloat16)
    grad_inputs = product("ecf,edf->ecd", grad_gate, weights[:, 0]) + product(
        "ecf,edf->ecd", grad_up, weights[:, 1]
    )
    return (grad_gate, grad_up, grad_inputs.astype(jnp.bfloat16))


def expert_weight_grads(inputs, hidden, grad_gate, grad_up, grad_result):
    return jnp.stack(
        [
            product("ecd,ecf->edf", inputs, grad_gate),
            product("ecd,ecf->edf", inputs, grad_up),
            product("ecd,ecf->edf", grad_result, hidden),
        ],
        axis=1,
    )


def plain_body(
    block_in,
    segments,
    routes,
    attn_gain,
    query_key_value_weight,
    q_gain,
    k_gain,
    w_out,
    ffn_gain,
    router,
    expert_weights,
    cotangent,
):
    tok = block_in.shape[0]
    width = block_in.shape[1]
    top = routes.shape[1]
    rep_count = lax.axis_size("rep")
    shard_count = lax.axis_size("shard")
    experts = expert_weights.shape[0] * rep_count * shard_count
    capacity = tok * top * 2 // experts
    shard_pos = lax.axis_index("shard")
    qkv_whole, out_whole = (
        lax.all_gather(query_key_value_weight, "shard", axis=0, tiled=True),
        lax.all_gather(w_out, "shard", axis=0, tiled=True),
    )
    inputs = block_in.astype(jnp.float32)
    scale_one = rms_scale(inputs)
    normed_one = (inputs * scale_one * attn_gain).astype(jnp.bfloat16)
    query_key_value = jnp.dot(normed_one, qkv_whole, preferred_element_type=jnp.float32)
    q_raw, unrotated_key, projected_value = split_heads(query_key_value)
    positions = shard_pos * tok + jnp.arange(tok, dtype=jnp.int32)
    cosine, sine = rope_tables(positions)
    q_scale, q_rot = norm_rope(q_raw, q_gain, cosine, sine)
    k_scale, k_rot = norm_rope(unrotated_key, k_gain, cosine, sine)
    keys_all, values_all = (
        lax.all_gather(k_rot, "shard", axis=0, tiled=True),
        lax.all_gather(projected_value.astype(jnp.bfloat16), "shard", axis=0, tiled=True),
    )
    query_seg = lax.dynamic_slice_in_dim(segments, shard_pos * tok, tok)
    key_pos = jnp.arange(segments.shape[0], dtype=jnp.int32)
    allowed = (query_seg[:, None] == segments[None, :]) & (key_pos[None, :] <= positions[:, None])
    attended_f, lse = attend_forward(q_rot, keys_all, values_all, allowed)
    attended = attended_f.astype(jnp.bfloat16)
    middle = inputs + jnp.dot(attended, out_whole, preferred_element_type=jnp.float32)
    scale_two = rms_scale(middle)
    normed_two = (middle * scale_two * ffn_gain).astype(jnp.bfloat16)
    weights, chosen, picked, total, gates = route_gates(normed_two, router, routes)
    index = route_index(routes, experts, capacity)
    upstream = cotangent.astype(jnp.float32)
    grad_rows = (
        (gates[:, :, None] * upstream[:, None, :]).astype(jnp.bfloat16).reshape(tok * top, width)
    )
    paired = jnp.concatenate([jnp.repeat(normed_two, top, axis=0), grad_rows], axis=1)
    buffer = dispatch(paired, index, experts, capacity)
    received = lax.all_to_all(buffer, ("rep", "shard"), split_axis=0, concat_axis=1, tiled=True)
    token_rows = received[:, :, :width]
    grads = received[:, :, width:]
    gate_pre, up_pre, hidden, result = expert_forward(token_rows, expert_weights)
    grad_gate, grad_up, grad_inner = expert_backward(expert_weights, gate_pre, up_pre, grads)
    grad_experts = expert_weight_grads(token_rows, hidden, grad_gate, grad_up, grads)
    outgoing = jnp.concatenate([result, grad_inner], axis=2)
    returned = lax.all_to_all(outgoing, ("rep", "shard"), split_axis=1, concat_axis=0, tiled=True)
    fetched = collect(returned, index).reshape(tok, top, 2 * width)
    expert_rows = fetched[:, :, :width].astype(jnp.float32)
    grad_from_experts = jnp.sum(fetched[:, :, width:].astype(jnp.float32), axis=1)
    block_out = (middle + jnp.sum(gates[:, :, None] * expert_rows, axis=1)).astype(jnp.bfloat16)
    grad_gates = jnp.sum(expert_rows * upstream[:, None, :], axis=2)
    grad_from_router, grad_router = route_gates_back(
        normed_two, router, weights, chosen, picked, total, grad_gates
    )
    grad_norm_two, grad_ffn_gain = rms_back(
        middle, scale_two, ffn_gain, grad_from_experts + grad_from_router
    )
    grad_middle = upstream + grad_norm_two
    grad_middle_b = grad_middle.astype(jnp.bfloat16)
    columns = attended
    grad_out = lax.psum_scatter(
        lax.dot_general(
            columns, grad_middle_b, (((0,), (0,)), ((), ())), preferred_element_type=jnp.float32
        ).astype(jnp.bfloat16),
        "shard",
        scatter_dimension=0,
        tiled=True,
    ).astype(jnp.float32)
    grad_attended = jnp.dot(grad_middle_b, out_whole.T, preferred_element_type=jnp.float32).astype(
        jnp.bfloat16
    )
    grad_q_rot, grad_k_all, grad_v_all = attend_backward(
        q_rot, keys_all, values_all, allowed, lse, attended, grad_attended
    )
    grad_k_rot, grad_v = (
        lax.psum_scatter(
            grad_k_all.astype(jnp.bfloat16), "shard", scatter_dimension=0, tiled=True
        ).astype(jnp.float32),
        lax.psum_scatter(
            grad_v_all.astype(jnp.bfloat16), "shard", scatter_dimension=0, tiled=True
        ).astype(jnp.float32),
    )
    grad_q_raw, grad_q_gain = norm_rope_back(q_raw, q_scale, q_gain, cosine, sine, grad_q_rot)
    grad_k_raw, grad_k_gain = norm_rope_back(
        unrotated_key, k_scale, k_gain, cosine, sine, grad_k_rot
    )
    grad_qkv_b = jnp.concatenate(
        [grad_q_raw.reshape(tok, -1), grad_k_raw.reshape(tok, -1), grad_v.reshape(tok, -1)], axis=1
    ).astype(jnp.bfloat16)
    columns = normed_one
    grad_qkv = lax.psum_scatter(
        lax.dot_general(
            columns, grad_qkv_b, (((0,), (0,)), ((), ())), preferred_element_type=jnp.float32
        ).astype(jnp.bfloat16),
        "shard",
        scatter_dimension=0,
        tiled=True,
    ).astype(jnp.float32)
    grad_norm_one = jnp.dot(grad_qkv_b, qkv_whole.T, preferred_element_type=jnp.float32)
    grad_inputs, grad_attn_gain = rms_back(inputs, scale_one, attn_gain, grad_norm_one)
    grad_input = (grad_middle + grad_inputs).astype(jnp.bfloat16)
    grad_attn_gain, grad_q_gain, grad_k_gain, grad_ffn_gain, grad_router = lax.psum(
        (grad_attn_gain, grad_q_gain, grad_k_gain, grad_ffn_gain, grad_router), ("rep", "shard")
    )
    grad_qkv, grad_out = (
        lax.psum(grad_qkv.astype(jnp.bfloat16), "rep").astype(jnp.float32),
        lax.psum(grad_out.astype(jnp.bfloat16), "rep").astype(jnp.float32),
    )
    return (
        block_out,
        grad_input,
        grad_attn_gain,
        grad_qkv,
        grad_q_gain,
        grad_k_gain,
        grad_out,
        grad_ffn_gain,
        grad_router,
        grad_experts,
    )


MESH_ID = pl.DeviceIdType.MESH
PLANES = 4


def place():
    rep, shard = lax.axis_index("rep"), lax.axis_index("shard")
    return rep // 2, rep % 2, shard // 2, shard % 2


def device(z, core, y, x):
    return (z * 2 + core, y * 2 + x)


def block_of(z, core, y, x):
    return (z * 2 + core) * 4 + y * 2 + x


def greet(targets):
    barrier = pltpu.get_barrier_semaphore()
    for condition, target in targets:
        if condition is None:
            pl.semaphore_signal(barrier, inc=1, device_id=target, device_id_type=MESH_ID)
        else:

            @pl.when(condition)
            def _():
                pl.semaphore_signal(barrier, inc=1, device_id=target, device_id_type=MESH_ID)

    peers = 0
    for condition, _ in targets:
        peers = peers + (1 if condition is None else condition.astype(jnp.int32))
    pl.semaphore_wait(barrier, peers)


def experts_kernel(
    x_ref,
    table_ref,
    upstream_ref,
    w_ref,
    x_all,
    table_all,
    out_ref,
    grad_ref,
    gg_ref,
    rows_out,
    hidden_out,
    gs,
    rows_hold,
    hidden_hold,
    x_hold,
    g_hold,
    t_hold,
    out_hold,
    grad_hold,
    send_sem,
    recv_sem,
    own_sem,
    load_sem,
    store_sem,
):
    ins, outs = (x_ref, table_ref), (x_all, table_all)
    rows = (x_ref.shape[0], table_ref.shape[0])
    count = len(ins)
    tok = rows[0]
    experts = rows[1] // 2
    z, core, y, x = place()
    partner = device(z, 1 - core, y, x)
    x_next, y_next = device(z, core, y, 1 - x), device(z, core, 1 - y, x)
    up, down = device(z + 1, core, y, x), device(z - 1, core, y, x)
    can_up, can_down = z < PLANES - 1, z > 0
    greet(
        [
            (None, partner),
            (None, x_next),
            (None, y_next),
            (can_up, up),
            (can_down, down),
        ]
    )
    tables = ((0, 1, 2, 3), (1, 0, 2, 3), (2, 3, 1, 0), (3, 2, 1, 0))
    order = [
        sum((z == level).astype(jnp.int32) * tables[level][n] for level in range(PLANES))
        for n in range(PLANES)
    ]
    pending, used = [], [0]

    def region(array, block, part):
        size = rows[array]
        if part is None:
            return pl.ds(pl.multiple_of(block * size, size), size)
        return pl.ds(pl.multiple_of(block * size + part * (size // 2), size // 2), size // 2)

    def copy_of(array, block, part, target, index, own=False):
        where = region(array, block, part)
        source = ins[array] if own else outs[array].at[where]
        return remote(
            source,
            outs[array].at[where],
            send_sem.at[array, index],
            recv_sem.at[array, block * 2 + (part or 0)],
            target,
        )

    def plan(block, part, target, condition=None, own=False):
        index = used[0]
        used[0] += 1

        def start():
            for array in range(count):
                copy_of(array, block, part, target, index, own).start()

        def finish():
            for array in range(count):
                copy_of(array, block, part, target, index, own).wait_send()

        pending.append((condition, finish))
        return lambda: start() if condition is None else pl.when(condition)(start)

    def arrived(block, part):
        for array in range(count):
            copy_of(array, block, part, partner, 0).wait_recv()

    own = block_of(z, core, y, x)
    for target, condition in (
        (up, can_up),
        (down, can_down),
        (x_next, None),
        (y_next, None),
        (partner, None),
    ):
        plan(own, None, target, condition, own=True)()
    locals_ = [
        pltpu.make_async_copy(ins[n], outs[n].at[region(n, own, None)], own_sem.at[n])
        for n in range(count)
    ]
    for copy in locals_:
        copy.start()

    def along(n):
        plane = order[n]
        block = block_of(plane, core, y, x)
        moves = [
            plan(block, None, up, jnp.logical_and(plane < z, can_up)),
            plan(block, None, down, jnp.logical_and(plane > z, can_down)),
            plan(block, None, x_next),
            plan(block, None, y_next),
            plan(block, None, partner),
        ]

        def run():
            arrived(block, None)
            for move in moves:
                move()

        return run

    def across(n):
        plane = order[n]
        from_x, from_y = block_of(plane, core, y, 1 - x), block_of(plane, core, 1 - y, x)
        moves = [
            plan(from_x, 1, y_next),
            plan(from_x, None, partner),
            plan(from_y, 0, x_next),
            plan(from_y, None, partner),
        ]

        def run():
            arrived(from_x, None)
            moves[0]()
            moves[1]()
            arrived(from_y, None)
            moves[2]()
            moves[3]()

        return run

    def diagonal(n):
        block = block_of(order[n], core, 1 - y, 1 - x)
        moves = [plan(block, part, partner) for part in range(2)]

        def run():
            for part in range(2):
                arrived(block, part)
                moves[part]()

        return run

    def paired(n):
        plane = order[n]

        def run():
            for where_y, where_x in ((y, x), (y, 1 - x), (1 - y, x)):
                arrived(block_of(plane, 1 - core, where_y, where_x), None)
            for part in range(2):
                arrived(block_of(plane, 1 - core, 1 - y, 1 - x), part)

        return run

    def settled():
        for copy in locals_:
            copy.wait()

    inside = jnp.logical_and(can_up, can_down)
    steps_along = [along(n) for n in range(1, PLANES)]

    def hop(n, condition):
        return lambda: pl.when(condition)(steps_along[n - 1])

    outside = jnp.logical_not(inside)
    work = (
        (across(0), steps_along[0], hop(2, inside), diagonal(0), settled),
        (across(1), hop(2, outside), hop(3, inside), paired(0)),
        (hop(3, outside), diagonal(1)),
        (across(2), paired(1)),
        (across(3), diagonal(2)),
        (diagonal(3), paired(2)),
        (),
        (paired(3),),
    )
    group = 4 * tok
    steps = len(work)
    cap = gs.shape[0] // 4
    me = block_of(z, core, y, x)

    def group_of(i):
        if isinstance(i, int):
            plane = order[i // 2]
        else:
            plane = sum((i // 2 == n).astype(jnp.int32) * order[n] for n in range(PLANES))
        return plane * 2 + (core + i % 2) % 2

    def group_rows(ref, i):
        return ref.at[pl.ds(pl.multiple_of(group_of(i) * group, group), group)]

    def load_g(i):
        return pltpu.make_async_copy(
            group_rows(upstream_ref, i), g_hold.at[i % 2], load_sem.at[i % 2]
        )

    def load_x(i):
        return pltpu.make_async_copy(group_rows(x_all, i), x_hold, load_sem.at[2])

    def load_t(i):
        size = 4 * rows[1]
        return pltpu.make_async_copy(
            table_all.at[pl.ds(pl.multiple_of(group_of(i) * size, size), size)],
            t_hold,
            load_sem.at[3],
        )

    def store(i):
        held = pl.ds(pl.multiple_of(i * 4 * cap, 4 * cap), 4 * cap)
        return [
            pltpu.make_async_copy(hold.at[i % 2], target, store_sem.at[n, i % 2])
            for n, (hold, target) in enumerate(
                (
                    (out_hold, group_rows(out_ref, i)),
                    (grad_hold, group_rows(grad_ref, i)),
                    (rows_hold, rows_out.at[:, held]),
                    (hidden_hold, hidden_out.at[:, held]),
                )
            )
        ]

    def dot(left, right, dims):
        return lax.dot_general(
            left, right, ((dims[:1], dims[1:]), ((), ())), preferred_element_type=jnp.float32
        )

    load_g(0).start()

    @pl.loop(0, steps)
    def _(i):
        for n in range(steps):
            if work[n]:

                @pl.when(i == n)
                def _():
                    for run in work[n]:
                        run()

        load_x(i).start()
        load_t(i).start()

        @pl.when(i + 1 < steps)
        def _():
            load_g(i + 1).start()

        @pl.when(i >= 2)
        def _():
            for copy in store(i - 2):
                copy.wait()

        load_t(i).wait()
        load_x(i).wait()
        load_g(i).wait()
        slot = i % 2
        chosen, gate_cols = [], []
        for pair in range(2):
            first = [(pair * 2 + j) * 2 * experts + me for j in range(2)]
            gate_row = jnp.concatenate([t_hold[pl.ds(at, 1), :] for at in first], axis=1)
            slot_row = jnp.concatenate(
                [
                    t_hold[pl.ds(at + experts, 1), :] + float(cap * j)
                    for j, at in enumerate(first)
                ],
                axis=1,
            )
            ids = lax.broadcasted_iota(jnp.int32, (2 * cap, 2 * tok), 0).astype(jnp.float32)
            mask = jnp.where(ids == slot_row, 1.0, 0.0)
            pick = mask.astype(jnp.bfloat16)
            held = pl.ds(pair * 2 * cap, 2 * cap)
            tokens = pl.ds(pair * 2 * tok, 2 * tok)
            gate = jnp.sum(mask * gate_row, axis=1, keepdims=True)
            rows_hold[slot, 0, held] = dot(pick, x_hold[tokens], (1, 0)).astype(jnp.bfloat16)
            upstream = dot(pick, g_hold[slot, tokens], (1, 0))
            gs[held] = upstream.astype(jnp.bfloat16)
            rows_hold[slot, 1, held] = (upstream * gate).astype(jnp.bfloat16)
            chosen.append(pick)
            gate_cols.append(gate)
        rows_x = rows_hold[slot, 0]
        rows_g = rows_hold[slot, 1]
        gate_pre = dot(rows_x, w_ref[0], (1, 0))
        up_pre = dot(rows_x, w_ref[1], (1, 0))
        sig = jax.nn.sigmoid(gate_pre)
        silu = gate_pre * sig
        hidden = (silu * up_pre).astype(jnp.bfloat16)
        grad_hidden = dot(rows_g, w_ref[2], (1, 0))
        grad_gate = (grad_hidden * up_pre * sig * (1.0 + gate_pre * (1.0 - sig))).astype(
            jnp.bfloat16
        )
        grad_up = (grad_hidden * silu).astype(jnp.bfloat16)
        result = dot(hidden, w_ref[2], (1, 1)).astype(jnp.bfloat16)
        grad_in = (dot(grad_gate, w_ref[0], (1, 1)) + dot(grad_up, w_ref[1], (1, 1))).astype(
            jnp.bfloat16
        )
        hidden_hold[slot, 0] = grad_gate
        hidden_hold[slot, 1] = grad_up
        hidden_hold[slot, 2] = hidden
        result_f = result.astype(jnp.float32)
        share = jnp.sum(gs[...].astype(jnp.float32) * result_f, axis=1, keepdims=True)
        for pair in range(2):
            tokens = pl.ds(pair * 2 * tok, 2 * tok)
            low, high = pair * 2 * cap, (pair + 1) * 2 * cap
            pick = chosen[pair]
            scaled = (result_f[low:high] * gate_cols[pair]).astype(jnp.bfloat16)
            out_hold[slot, tokens] = dot(pick, scaled, (0, 0)).astype(jnp.bfloat16)
            grad_hold[slot, tokens] = dot(pick, grad_in[low:high], (0, 0)).astype(jnp.bfloat16)
            row = jnp.sum(pick.astype(jnp.float32) * share[low:high], axis=0, keepdims=True)
            for j in range(2):
                gg_ref[pl.ds(group_of(i) * 4 + pair * 2 + j, 1), :] = row[
                    :, j * tok : (j + 1) * tok
                ]
        for copy in store(i):
            copy.start()

    for i in (steps - 2, steps - 1):
        for copy in store(i):
            copy.wait()
    for condition, finish in pending:
        if condition is None:
            finish()
        else:
            pl.when(condition)(finish)


def run_experts(tokens, table, upstream, weights, cap, collective_id):
    tok, width = tokens.shape
    _, three, _, ff = weights.shape
    devices = 32
    total = tok * devices
    held = 4 * cap
    group = 4 * tok
    return pl.pallas_call(
        experts_kernel,
        out_shape=[
            jax.ShapeDtypeStruct((total, width), tokens.dtype),
            jax.ShapeDtypeStruct((table.shape[0] * devices, tok), table.dtype),
            jax.ShapeDtypeStruct((total, width), jnp.bfloat16),
            jax.ShapeDtypeStruct((total, width), jnp.bfloat16),
            jax.ShapeDtypeStruct((devices, tok), jnp.float32),
            jax.ShapeDtypeStruct((2, 8 * held, width), jnp.bfloat16),
            jax.ShapeDtypeStruct((3, 8 * held, ff), jnp.bfloat16),
        ],
        in_specs=[
            pl.BlockSpec(memory_space=pltpu.VMEM),
            pl.BlockSpec(memory_space=pltpu.VMEM),
            pl.BlockSpec(memory_space=pltpu.HBM),
            pl.BlockSpec(memory_space=pltpu.VMEM),
        ],
        out_specs=[pl.BlockSpec(memory_space=pltpu.HBM)] * 4
        + [pl.BlockSpec(memory_space=pltpu.VMEM)]
        + [pl.BlockSpec(memory_space=pltpu.HBM)] * 2,
        scratch_shapes=[
            pltpu.VMEM((held, width), jnp.bfloat16),
            pltpu.VMEM((2, 2, held, width), jnp.bfloat16),
            pltpu.VMEM((2, 3, held, ff), jnp.bfloat16),
            pltpu.VMEM((group, width), jnp.bfloat16),
            pltpu.VMEM((2, group, width), jnp.bfloat16),
            pltpu.VMEM((4 * table.shape[0], tok), jnp.float32),
            pltpu.VMEM((2, group, width), jnp.bfloat16),
            pltpu.VMEM((2, group, width), jnp.bfloat16),
            pltpu.SemaphoreType.DMA((2, 44)),
            pltpu.SemaphoreType.DMA((2, 64)),
            pltpu.SemaphoreType.DMA((2,)),
            pltpu.SemaphoreType.DMA((4,)),
            pltpu.SemaphoreType.DMA((4, 2)),
        ],
        compiler_params=pltpu.CompilerParams(
            collective_id=collective_id, has_side_effects=True, vmem_limit_bytes=63 << 20
        ),
        name="run_experts",
    )(tokens, table, upstream, weights.reshape(three, width, ff))


def add_rows(target, sources, rows=128, step=16):
    @pl.loop(0, rows // step)
    def _(i):
        where = pl.ds(pl.multiple_of(i * step, step), step)
        total = target[where].astype(jnp.float32)
        for source in sources:
            total += source[where].astype(jnp.float32)
        target[where] = total.astype(target.dtype)


def rolled(values):
    return pltpu.roll(values, HEAD_SIZE // 2, 1)


def inverse_rms(values):
    return lax.rsqrt(jnp.mean(values * values, axis=1, keepdims=True) + epsilon)


def mm(left, right, dims):
    return lax.dot_general(
        left, right, ((dims[:1], dims[1:]), ((), ())), preferred_element_type=jnp.float32
    )


def fill_bias(bias, seg_col, seg_row):
    seq = bias.shape[0]
    key = lax.broadcasted_iota(jnp.int32, (seq, seq), 0)
    query = lax.broadcasted_iota(jnp.int32, (seq, seq), 1)
    same = seg_col[...] == seg_row[...]
    bias[...] = jnp.where(jnp.logical_and(same, key <= query), 0.0, -1e30)


def attend_kernel(
    x_ref,
    weight_ref,
    w_out_ref,
    gain_ref,
    q_gain_ref,
    k_gain_ref,
    cos_ref,
    sin_ref,
    seg_col,
    seg_row,
    normed_ref,
    raw_ref,
    q_ref,
    k_ref,
    v_ref,
    attended_ref,
    lse_ref,
    part_ref,
    bias,
):
    seq = x_ref.shape[0]
    size = HEAD_SIZE
    heads = q_ref.shape[1] // size
    scale = size ** (-0.5)

    @pl.loop(0, seq // 64)
    def _(n):
        rows = pl.ds(pl.multiple_of(n * 64, 64), 64)
        x = x_ref[rows].astype(jnp.float32)
        normed_ref[rows] = (x * inverse_rms(x) * gain_ref[...]).astype(jnp.bfloat16)

    fill_bias(bias, seg_col, seg_row)

    @pl.loop(0, raw_ref.shape[1] // 256)
    def _(n):
        columns = pl.ds(pl.multiple_of(n * 256, 256), 256)
        raw_ref[:, columns] = mm(normed_ref[...], weight_ref[:, columns], (1, 0))

    def turned(raw, gain_row):
        normed = raw * inverse_rms(raw) * gain_row
        return (normed * cos_ref[...] + rolled(normed) * sin_ref[...]).astype(jnp.bfloat16)

    k_ref[...] = turned(raw_ref[:, heads * size : (heads + 1) * size], k_gain_ref[...])
    v_ref[...] = raw_ref[:, (heads + 1) * size :].astype(jnp.bfloat16)
    half = seq // 2

    @pl.loop(0, heads)
    def _(h):
        columns = pl.ds(pl.multiple_of(h * size, size), size)
        q_ref[:, columns] = turned(raw_ref[:, columns], q_gain_ref[...])
        for first, keys in ((0, half), (half, seq)):
            queries = pl.ds(first, half)
            score = mm(k_ref[:keys], q_ref[queries, columns], (1, 1)) * scale
            score = score + bias[:keys, first : first + half]
            highest = jnp.max(score, axis=0, keepdims=True)
            power = jnp.exp(score - highest)
            total = jnp.sum(power, axis=0, keepdims=True)
            lse_ref[pl.ds(h, 1), queries] = highest + jnp.log(total)
            probs = (power * (1.0 / total)).astype(jnp.bfloat16)
            attended_ref[queries, columns] = mm(probs, v_ref[:keys], (0, 0)).astype(jnp.bfloat16)

    @pl.loop(0, part_ref.shape[1] // 512)
    def _(n):
        columns = pl.ds(pl.multiple_of(n * 512, 512), 512)
        part_ref[:, columns] = mm(attended_ref[...], w_out_ref[:, columns], (1, 0)).astype(
            jnp.bfloat16
        )


def attend(x, weight, w_out, gain, q_gain, k_gain, cosine, sine, segments):
    seq, width = x.shape
    columns = weight.shape[1]
    heads = w_out.shape[0] // HEAD_SIZE
    bf, f4 = jnp.bfloat16, jnp.float32
    out = jax.ShapeDtypeStruct
    return pl.pallas_call(
        attend_kernel,
        out_shape=[
            out((seq, width), bf),
            out((seq, columns), f4),
            out((seq, heads * HEAD_SIZE), bf),
            out((seq, HEAD_SIZE), bf),
            out((seq, HEAD_SIZE), bf),
            out((seq, heads * HEAD_SIZE), bf),
            out((heads, seq), f4),
            out((seq, width), bf),
        ],
        in_specs=[pl.BlockSpec(memory_space=pltpu.VMEM)] * 10,
        out_specs=[pl.BlockSpec(memory_space=pltpu.VMEM)] * 8,
        scratch_shapes=[pltpu.VMEM((seq, seq), f4)],
        compiler_params=pltpu.CompilerParams(vmem_limit_bytes=56 << 20),
        name="attend",
    )(
        x,
        weight,
        w_out,
        gain[None],
        q_gain[None],
        k_gain[None],
        cosine,
        sine,
        segments[:, None],
        segments[None],
    )


def backward_steps(refs):
    q_ref, k_ref, v_ref, raw_ref, upstream, lse_ref, delta_ref = refs[:7]
    q_gain_ref, k_gain_ref, cos_ref, sin_ref, seg_col, seg_row = refs[7:13]
    grad_ref, gains_ref, bias, grad_k, grad_v = refs[13:]
    seq, size = k_ref.shape
    heads = q_ref.shape[1] // size
    scale = size ** (-0.5)
    half = seq // 2

    def prepare():
        fill_bias(bias, seg_col, seg_row)
        grad_k[...] = jnp.zeros_like(grad_k)
        grad_v[...] = jnp.zeros_like(grad_v)
        gains_ref[...] = jnp.zeros_like(gains_ref)

    def turn_back(grad, queries, columns, gain, line):
        turned = grad * cos_ref[queries] + rolled(grad * sin_ref[queries])
        raw = raw_ref[queries, columns]
        inverse = inverse_rms(raw)
        scaled = turned * gain
        mean = jnp.mean(scaled * raw, axis=1, keepdims=True)
        grad_raw = inverse * scaled - raw * (inverse * inverse * inverse) * mean
        grad_ref[queries, columns] = grad_raw.astype(jnp.bfloat16)
        gains_ref[line : line + 1] += jnp.sum(turned * raw * inverse, axis=0, keepdims=True)

    def head(h):
        columns = pl.ds(h * size, size)
        for first, keys in ((0, half), (half, seq)):
            queries = pl.ds(first, half)
            q, above = q_ref[queries, columns], upstream[queries, columns]
            score = mm(k_ref[:keys], q, (1, 1)) * scale + bias[:keys, first : first + half]
            probs = jnp.exp(score - lse_ref[h : h + 1, first : first + half])
            grad_v[:keys] += mm(probs.astype(jnp.bfloat16), above, (1, 0))
            grad_p = mm(v_ref[:keys], above, (1, 1))
            delta = delta_ref[h : h + 1, first : first + half]
            grad_score = (probs * (grad_p - delta) * scale).astype(jnp.bfloat16)
            grad_k[:keys] += mm(grad_score, q, (1, 0))
            grad_q = mm(grad_score, k_ref[:keys], (0, 0))
            turn_back(grad_q, queries, columns, q_gain_ref[...], 0)

    def keys_and_values():
        for first in (0, half):
            queries = pl.ds(first, half)
            turn_back(grad_k[queries], queries, pl.ds(heads * size, size), k_gain_ref[...], 1)
        grad_ref[:, (heads + 1) * size :] = grad_v[...].astype(jnp.bfloat16)

    return [prepare] + [functools.partial(head, h) for h in range(heads)] + [keys_and_values]


class Sends:
    def __init__(self, send_sem, partner):
        self.send_sem, self.partner, self.used, self.pending = send_sem, partner, 0, []

    def make(self, source, landing, sem, target, *conditions):
        copy = remote(source, landing, self.send_sem.at[self.used], sem, target)
        self.used += 1
        self.pending.append((conditions, copy))
        return copy

    def send(self, source, landing, sem, target):
        self.make(source, landing, sem, target).start()

    def arrived(self, landing, sem):
        remote(landing, landing, self.send_sem.at[0], sem, self.partner).wait_recv()

    def finish(self):
        for conditions, copy in self.pending:
            if not conditions:
                copy.wait_send()
            elif len(conditions) == 1:
                pl.when(conditions[0])(copy.wait_send)
            else:
                pl.when(jnp.logical_and(*conditions))(copy.wait_send)


def add_into(target, sources, rows):
    @pl.loop(0, rows // 16)
    def _(n):
        where = pl.ds(pl.multiple_of(n * 16, 16), 16)
        total = sources[0][where].astype(jnp.float32)
        for source in sources[1:]:
            total += source[where].astype(jnp.float32)
        target[where] = total.astype(target.dtype)


def ladder(sends, count, before, piece, from_up, from_down, final, size, sems):
    climb_send, spread_send, close_send, climb_sem, spread_sem, close_sem = sems
    z, core, y, x = place()
    partner = sends.partner
    up, down = device(z + 1, core, y, x), device(z - 1, core, y, x)
    can_up, can_down = z < PLANES - 1, z > 0

    def climb(n, rising):
        landing = from_down(n) if rising else from_up(n)
        side = 1 if rising else 0
        return remote(
            piece(n), landing, climb_send.at[n], climb_sem.at[n, side], up if rising else down
        )

    def gained(n, rising):
        landing = from_down(n) if rising else from_up(n)
        sends.arrived(landing, climb_sem.at[n, 1 if rising else 0])
        return landing

    def spread(n, rising):
        block = final(n, core)
        target = up if rising else down
        return remote(block, block, spread_send.at[n, 1 if rising else 0], spread_sem.at[n], target)

    def hand_over(n):
        block = final(n, core)
        return remote(block, block, close_send.at[n], close_sem.at[n], partner)

    def ends(n, root):
        before(n)
        pl.when(z == 0)(climb(n, True).start)
        pl.when(z == PLANES - 1)(climb(n, False).start)

    def between(n, root):
        for rising, level in ((True, 1), (False, 2)):

            @pl.when(jnp.logical_and(z == level, root == 3 - level))
            def _():
                add_rows(piece(n), (gained(n, rising),), size)
                climb(n, rising).start()

    def settle(n, root):
        @pl.when(z == root)
        def _():
            add_into(final(n, core), (piece(n), gained(n, True), gained(n, False)), size)
            spread(n, True).start()
            spread(n, False).start()
            hand_over(n).start()

    def receive(n, root, distance):
        for rising, there, more in (
            (True, z == root + distance, can_up),
            (False, z == root - distance, can_down),
        ):

            @pl.when(there)
            def _():
                sends.arrived(final(n, core), spread_sem.at[n])
                pl.when(more)(spread(n, rising).start)
                hand_over(n).start()

    stages = (
        ends,
        between,
        settle,
        functools.partial(receive, distance=1),
        functools.partial(receive, distance=2),
    )

    def step(m):
        for stage, run in enumerate(stages):
            n = m - stage * SLACK

            @pl.when(jnp.logical_and(n >= 0, n < count))
            def _():
                run(n, 1 + n % 2)

    def close():
        @pl.loop(0, count)
        def _(n):
            root = 1 + n % 2
            pl.when(z != root)(climb(n, True).wait_send)
            pl.when(jnp.logical_and(z >= root, can_up))(spread(n, True).wait_send)
            pl.when(jnp.logical_and(z <= root, can_down))(spread(n, False).wait_send)
            hand_over(n).wait_send()

    def closed(n):
        sends.arrived(final(n, 1 - core), close_sem.at[n])

    return step, closed, close


SLACK = 2
LADDER_MORE = 4 * SLACK


def ladder_scratch(count):
    return [
        pltpu.SemaphoreType.DMA((count,)),
        pltpu.SemaphoreType.DMA((count, 2)),
        pltpu.SemaphoreType.DMA((count,)),
        pltpu.SemaphoreType.DMA((count, 2)),
        pltpu.SemaphoreType.DMA((count,)),
        pltpu.SemaphoreType.DMA((count,)),
    ]


LADDER = 32
PER = LADDER // 4


def reduce_kernel(with_weight, *refs):
    refs = list(refs)
    part_ref = refs.pop(0)
    weight_ref = refs.pop(0) if with_weight else None
    back = [refs.pop(0) for _ in range(13)] if with_weight else []
    rows_ref, hidden_ref = (None, None) if with_weight else (refs.pop(0), refs.pop(0))
    out_ref = refs.pop(0)
    weight_out = refs.pop(0) if with_weight else None
    grad_w = None if with_weight else refs.pop(0)
    back += [refs.pop(0) for _ in range(2)] if with_weight else []
    kept, paired, x_half, x_full, y_half, y_full, from_up, from_down = refs[:8]
    send_sem, pair_sem, x_sem, y_sem, z_sem, load_sem = refs[8:14]
    rows = out_ref.shape[0]
    half = rows // 2
    z, core, y, x = place()
    partner = device(z, 1 - core, y, x)
    x_next, y_next = device(z, core, y, 1 - x), device(z, core, 1 - y, x)
    up, down = device(z + 1, core, y, x), device(z - 1, core, y, x)
    greet(
        [
            (None, partner),
            (None, x_next),
            (None, y_next),
            (z < PLANES - 1, up),
            (z > 0, down),
        ]
    )
    sends = Sends(send_sem, partner)
    tables = ((3, 2, 1, 0), (3, 0, 2, 1), (0, 3, 1, 2), (0, 1, 2, 3))
    order = [
        sum((z == level).astype(jnp.int32) * tables[level][n] for level in range(PLANES))
        for n in range(PLANES)
    ]
    spots = ((1 - y, 1 - x), (y, 1 - x), (1 - y, x), (y, x))

    def slot(plane, spot):
        return plane * 4 + spots[spot][0] * 2 + spots[spot][1]

    def block(plane, which, spot):
        size = pl.multiple_of(block_of(plane, which, *spots[spot]) * rows, rows)
        return part_ref.at[pl.ds(size, rows)]

    def load(plane, spot):
        return pltpu.make_async_copy(
            block(plane, core, spot), kept.at[slot(plane, spot)], load_sem.at[spot * 4 + plane]
        )

    for spot in range(4):
        for plane in order:
            where = slot(plane, spot)
            sends.send(block(plane, 1 - core, spot), paired.at[where], pair_sem.at[where], partner)
            load(plane, spot).start()
    if with_weight:
        out_pair, out_part, out_up, out_down, out_done = refs[14:19]
        out_pair_sem, out_sem = refs[19:21]
        out_half = weight_ref.shape[0] // 2
        out_block = out_half // LADDER
        big = out_half // 4

        def out_rows(n, which, count=1):
            start = pl.multiple_of(which * out_half + n * out_block, out_block)
            return weight_ref.at[pl.ds(start, out_block * count)]

        for n in range(4):
            sends.send(out_rows(n * PER, 1 - core, PER), out_pair.at[n], out_pair_sem.at[n], partner)

        def before(n):
            @pl.when(n % PER == 0)
            def _():
                where = n // PER
                sends.arrived(out_pair.at[where], out_pair_sem.at[where])
                add_into(out_part.at[where], (out_rows(n, core, PER), out_pair.at[where]), big)

        def done_rows(n, which):
            start = pl.multiple_of(which * out_half + n * out_block, out_block)
            return out_done.at[pl.ds(start, out_block)]

        ladder_step, closed, close = ladder(
            sends,
            LADDER,
            before,
            lambda n: out_part.at[
                n // PER, pl.ds(pl.multiple_of((n % PER) * out_block, out_block), out_block)
            ],
            lambda n: out_up.at[n],
            lambda n: out_down.at[n],
            done_rows,
            out_block,
            refs[21:27],
        )
        fill = backward_steps(back + refs[27:])

    else:
        rows_hold, hidden_hold, sums, part_sem, sum_sem = refs[14:]
        held = rows_hold.shape[2]

        def fetch(i):
            span = pl.ds(i * held, held)
            return (
                pltpu.make_async_copy(
                    rows_ref.at[:, span], rows_hold.at[i % 2], part_sem.at[0, i % 2]
                ),
                pltpu.make_async_copy(
                    hidden_ref.at[:, span], hidden_hold.at[i % 2], part_sem.at[1, i % 2]
                ),
            )

        parts = rows_ref.shape[1] // held
        for copy in fetch(0):
            copy.start()

        def add_product(i):
            if i + 1 < parts:
                for copy in fetch(i + 1):
                    copy.start()
            for copy in fetch(i):
                copy.wait()
            for matrix, source in ((0, 0), (1, 0), (2, 1)):

                @pl.loop(0, sums.shape[1] // 512)
                def _(n):
                    span = pl.ds(pl.multiple_of(n * 512, 512), 512)
                    product = mm(
                        rows_hold[i % 2, source, :, span], hidden_hold[i % 2, matrix], (0, 0)
                    )
                    if i:
                        sums[matrix, span] += product
                    else:
                        sums[matrix, span] = product

        write_sums = pltpu.make_async_copy(sums, grad_w.at[0], sum_sem)

    def joined(plane, spot, more=()):
        where = slot(plane, spot)
        load(plane, spot).wait()
        sends.arrived(paired.at[where], pair_sem.at[where])
        add_rows(kept.at[where], (paired.at[where],) + tuple(more), rows)

    def across(plane):
        joined(plane, 0)
        source = kept.at[slot(plane, 0)]
        sends.send(source.at[pl.ds(0, half)], x_half.at[plane], x_sem.at[plane], x_next)
        sends.send(source.at[pl.ds(half, half)], y_half.at[plane], y_sem.at[plane], y_next)

    def beside(plane):
        joined(plane, 1)
        sends.arrived(y_half.at[plane], y_sem.at[plane])
        add_rows(kept.at[slot(plane, 1)].at[pl.ds(half, half)], (y_half.at[plane],), half)
        sends.send(kept.at[slot(plane, 1)], x_full.at[plane], x_sem.at[4 + plane], x_next)
        joined(plane, 2)
        sends.arrived(x_half.at[plane], x_sem.at[plane])
        add_rows(kept.at[slot(plane, 2)].at[pl.ds(0, half)], (x_half.at[plane],), half)
        sends.send(kept.at[slot(plane, 2)], y_full.at[plane], y_sem.at[4 + plane], y_next)

    def along(plane):
        sends.arrived(x_full.at[plane], x_sem.at[4 + plane])
        sends.arrived(y_full.at[plane], y_sem.at[4 + plane])
        joined(plane, 3, (x_full.at[plane], y_full.at[plane]))

    moves = {}

    def pass_on(n, first):
        plane = order[n]
        total = kept.at[slot(plane, 3)]
        if first:
            fall = sends.make(total, from_up.at[plane], z_sem.at[0, plane], down, z > plane)
            rise = sends.make(total, from_down.at[plane], z_sem.at[1, plane], up, z < plane)
            moves[n] = (fall, rise)
        fall, rise = moves[n]
        for copy, way, end, landing, sem in (
            (fall, z > plane, z == PLANES - 1, from_up.at[plane], z_sem.at[0, plane]),
            (rise, z < plane, z == 0, from_down.at[plane], z_sem.at[1, plane]),
        ):
            if first:
                pl.when(jnp.logical_and(way, end))(copy.start)
            else:

                @pl.when(jnp.logical_and(way, jnp.logical_not(end)))
                def _():
                    sends.arrived(landing, sem)
                    add_rows(total, (landing,), rows)
                    copy.start()

    total_steps = LADDER + LADDER_MORE
    done_steps = 0
    if with_weight:
        fill[0]()
    for late, run in enumerate((across, beside)):
        for n, plane in enumerate(order):
            run(plane)
            if not with_weight:
                add_product(late * PLANES + n)
            if with_weight:
                if run is across:
                    fill[1 + n]()
                more = min(-(-total_steps // (2 * PLANES)), total_steps - done_steps)

                @pl.loop(done_steps, done_steps + more)
                def _(m):
                    ladder_step(m)

                done_steps += more
    if not with_weight:
        write_sums.start()
    for n in range(PLANES):
        along(order[n])
        if n < PLANES - 1:
            pass_on(n, True)
        if n:
            pass_on(n - 1, False)
        if with_weight:
            fill[1 + PLANES + n]()
    if with_weight:
        fill[-1]()
    mine = kept.at[slot(z, 3)]

    @pl.when(z < PLANES - 1)
    def _():
        sends.arrived(from_up.at[z], z_sem.at[0, z])
        add_rows(mine, (from_up.at[z],), rows)

    @pl.when(z > 0)
    def _():
        sends.arrived(from_down.at[z], z_sem.at[1, z])
        add_rows(mine, (from_down.at[z],), rows)

    out_ref[...] = mine[...]
    if with_weight:

        @pl.loop(0, LADDER)
        def _(n):
            closed(n)

        write = pltpu.make_async_copy(out_done, weight_out, out_sem)
        write.start()
        close()
        write.wait()
    else:
        write_sums.wait()
    sends.finish()


def reduce_all(part, collective_id, weight=None, back=(), expert=()):
    total, width = part.shape
    rows = total // 32
    half = rows // 2
    dtype = part.dtype
    out_shape = [jax.ShapeDtypeStruct((rows, width), dtype)]
    in_specs = [pl.BlockSpec(memory_space=pltpu.HBM)]
    out_specs = [pl.BlockSpec(memory_space=pltpu.VMEM)]
    scratch = [
        pltpu.VMEM((16, rows, width), dtype),
        pltpu.VMEM((16, rows, width), dtype),
        pltpu.VMEM((4, half, width), dtype),
        pltpu.VMEM((4, rows, width), dtype),
        pltpu.VMEM((4, half, width), dtype),
        pltpu.VMEM((4, rows, width), dtype),
        pltpu.VMEM((4, rows, width), dtype),
        pltpu.VMEM((4, rows, width), dtype),
        pltpu.SemaphoreType.DMA((52,)),
        pltpu.SemaphoreType.DMA((16,)),
        pltpu.SemaphoreType.DMA((8,)),
        pltpu.SemaphoreType.DMA((8,)),
        pltpu.SemaphoreType.DMA((2, 4)),
        pltpu.SemaphoreType.DMA((16,)),
    ]
    operands = [part]
    if weight is not None:
        operands.append(weight)
        block = weight.shape[0] // 8
        seq = back[0].shape[0]
        operands += back
        out_shape += [
            jax.ShapeDtypeStruct(weight.shape, dtype),
            jax.ShapeDtypeStruct(back[3].shape, dtype),
            jax.ShapeDtypeStruct((8, HEAD_SIZE), jnp.float32),
        ]
        in_specs += [pl.BlockSpec(memory_space=pltpu.VMEM)] * (1 + len(back))
        out_specs += [
            pl.BlockSpec(memory_space=pltpu.HBM),
            pl.BlockSpec(memory_space=pltpu.VMEM),
            pl.BlockSpec(memory_space=pltpu.VMEM),
        ]
        scratch += [
            pltpu.VMEM((4, block, width), dtype),
            pltpu.VMEM((4, block, width), dtype),
            pltpu.VMEM((LADDER, weight.shape[0] // 2 // LADDER, width), dtype),
            pltpu.VMEM((LADDER, weight.shape[0] // 2 // LADDER, width), dtype),
            pltpu.VMEM(weight.shape, dtype),
            pltpu.SemaphoreType.DMA((4,)),
            pltpu.SemaphoreType.DMA,
        ] + ladder_scratch(LADDER)
        scratch += [
            pltpu.VMEM((seq, seq), jnp.float32),
            pltpu.VMEM((seq, HEAD_SIZE), jnp.float32),
            pltpu.VMEM((seq, HEAD_SIZE), jnp.float32),
        ]
    else:
        rows_held, hidden_held = expert
        held, ff = rows_held.shape[1] // 8, hidden_held.shape[2]
        operands += expert
        in_specs += [pl.BlockSpec(memory_space=pltpu.HBM)] * 2
        out_shape.append(jax.ShapeDtypeStruct((1, 3, width, ff), jnp.float32))
        out_specs.append(pl.BlockSpec(memory_space=pltpu.HBM))
        scratch += [
            pltpu.VMEM((2, 2, held, width), dtype),
            pltpu.VMEM((2, 3, held, ff), dtype),
            pltpu.VMEM((3, width, ff), jnp.float32),
            pltpu.SemaphoreType.DMA((2, 2)),
            pltpu.SemaphoreType.DMA,
        ]
    return pl.pallas_call(
        functools.partial(reduce_kernel, weight is not None),
        out_shape=out_shape,
        in_specs=in_specs,
        out_specs=out_specs,
        scratch_shapes=scratch,
        compiler_params=pltpu.CompilerParams(
            collective_id=collective_id, has_side_effects=True, vmem_limit_bytes=63 << 20
        ),
        name="reduce_all",
    )(*operands)


def others():
    z, core, y, x = place()
    return [
        (device(z, core, yy, xx), yy * 2 + xx)
        for yy, xx in ((y, 1 - x), (1 - y, x), (1 - y, 1 - x))
    ]


def remote(source, landing, send_sem, recv_sem, target):
    return pltpu.make_async_remote_copy(
        src_ref=source,
        dst_ref=landing,
        send_sem=send_sem,
        recv_sem=recv_sem,
        device_id=target,
        device_id_type=MESH_ID,
    )


def start_kernel(
    x_ref, w_ref, x_all, w_own, hold, send_sem, x_sem, w_sem, pair_sem, own_sem
):
    tok = x_ref.shape[0]
    depth = w_ref.shape[0]
    half = depth // 2
    z, core, y, x = place()
    me = y * 2 + x
    partner = device(z, 1 - core, y, x)
    near = others()
    greet([(None, target) for target, _ in near] + [(None, partner)])
    parts = QUERY_HEADS // 4 * HEAD_SIZE
    single = HEAD_SIZE
    widths = (
        (0, parts, 0),
        (QUERY_HEADS * HEAD_SIZE, single, parts),
        ((QUERY_HEADS + KEY_VALUE_HEADS) * HEAD_SIZE, single, parts + single),
    )

    def columns(piece, who):
        base, width, _ = widths[piece]
        return pl.ds(pl.multiple_of(base + who * width, 128), width)

    def landing(piece, who, part, ref=w_own):
        _, width, offset = widths[piece]
        rows = pl.ds(pl.multiple_of(who * depth + part * half, half), half)
        return ref.at[rows, pl.ds(offset, width)]

    sends = []
    for slot, (target, who) in enumerate(near):
        for piece in range(3):
            copy = remote(
                w_ref.at[pl.ds(pl.multiple_of(core * half, half), half), columns(piece, who)],
                landing(piece, me, core),
                send_sem.at[slot * 4 + piece],
                w_sem.at[slot * 3 + piece],
                target,
            )
            copy.start()
            sends.append(copy)
        copy = remote(
            x_ref,
            x_all.at[pl.ds(pl.multiple_of(me * tok, tok), tok)],
            send_sem.at[slot * 4 + 3],
            x_sem.at[slot],
            target,
        )
        copy.start()
        sends.append(copy)
    mine = pltpu.make_async_copy(
        x_ref, x_all.at[pl.ds(pl.multiple_of(me * tok, tok), tok)], own_sem.at[0]
    )
    mine.start()
    loads = []
    for piece in range(3):
        _, width, offset = widths[piece]
        loads.append(
            pltpu.make_async_copy(
                w_ref.at[:, columns(piece, me)], hold.at[:, pl.ds(offset, width)], own_sem.at[1 + piece]
            )
        )
        loads[-1].start()
    for copy in loads:
        copy.wait()
    keep = pltpu.make_async_copy(
        hold, w_own.at[pl.ds(pl.multiple_of(me * depth, depth), depth)], own_sem.at[4]
    )
    keep.start()
    for slot, (target, who) in enumerate(near):
        for piece in range(3):
            where = landing(piece, who, core)
            remote(where, where, send_sem.at[0], w_sem.at[slot * 3 + piece], partner).wait_recv()
        rows = w_own.at[pl.ds(pl.multiple_of(who * depth + core * half, half), half)]
        copy = remote(rows, rows, send_sem.at[12 + slot], pair_sem.at[slot], partner)
        copy.start()
        sends.append(copy)
    for slot, (target, who) in enumerate(near):
        rows = w_own.at[pl.ds(pl.multiple_of(who * depth + (1 - core) * half, half), half)]
        remote(rows, rows, send_sem.at[0], pair_sem.at[slot], partner).wait_recv()
        rows = x_all.at[pl.ds(pl.multiple_of(who * tok, tok), tok)]
        remote(rows, rows, send_sem.at[0], x_sem.at[slot], partner).wait_recv()
    mine.wait()
    keep.wait()
    for copy in sends:
        copy.wait_send()


def start_exchange(block_in, weight, collective_id):
    tok, width = block_in.shape
    depth, columns = weight.shape
    return pl.pallas_call(
        start_kernel,
        out_shape=[
            jax.ShapeDtypeStruct((tok * 4, width), block_in.dtype),
            jax.ShapeDtypeStruct((depth * 4, columns // 4), weight.dtype),
        ],
        in_specs=[
            pl.BlockSpec(memory_space=pltpu.VMEM),
            pl.BlockSpec(memory_space=pltpu.HBM),
        ],
        out_specs=[pl.BlockSpec(memory_space=pltpu.HBM)] * 2,
        scratch_shapes=[
            pltpu.VMEM((depth, columns // 4), weight.dtype),
            pltpu.SemaphoreType.DMA((16,)),
            pltpu.SemaphoreType.DMA((3,)),
            pltpu.SemaphoreType.DMA((9,)),
            pltpu.SemaphoreType.DMA((3,)),
            pltpu.SemaphoreType.DMA((5,)),
        ],
        compiler_params=pltpu.CompilerParams(
            collective_id=collective_id, has_side_effects=True, vmem_limit_bytes=40 << 20
        ),
        name="start_exchange",
    )(block_in, weight)


def spread_kernel(x_ref, x_all, send_sem, x_sem, own_sem):
    tok = x_ref.shape[0]
    z, core, y, x = place()
    me = y * 2 + x
    near = others()
    greet([(None, target) for target, _ in near[:2]])
    sends = Sends(send_sem, near[0][0])

    def rows(who, part=None):
        if part is None:
            return x_all.at[pl.ds(pl.multiple_of(who * tok, tok), tok)]
        start = who * tok + part * (tok // 2)
        return x_all.at[pl.ds(pl.multiple_of(start, tok // 2), tok // 2)]

    for slot in range(2):
        for part in (1 - slot, slot):
            sends.send(
                x_ref.at[pl.ds(part * (tok // 2), tok // 2)],
                rows(me, part),
                x_sem.at[slot, part],
                near[slot][0],
            )
    own_x = pltpu.make_async_copy(x_ref, rows(me), own_sem)
    own_x.start()
    for slot in range(2):
        who, part = near[slot][1], 1 - slot
        sends.arrived(rows(who, part), x_sem.at[slot, part])
        sends.send(rows(who, part), rows(who, part), x_sem.at[2, part], near[1 - slot][0])
    for slot in range(2):
        sends.arrived(rows(near[slot][1], slot), x_sem.at[slot, slot])
    for part in range(2):
        sends.arrived(rows(near[2][1], part), x_sem.at[2, part])
    own_x.wait()
    sends.finish()


def spread_sequence(rows, collective_id):
    tok, width = rows.shape
    return pl.pallas_call(
        spread_kernel,
        out_shape=jax.ShapeDtypeStruct((tok * 4, width), rows.dtype),
        in_specs=[pl.BlockSpec(memory_space=pltpu.VMEM)],
        out_specs=pl.BlockSpec(memory_space=pltpu.HBM),
        scratch_shapes=[
            pltpu.SemaphoreType.DMA((6,)),
            pltpu.SemaphoreType.DMA((3, 2)),
            pltpu.SemaphoreType.DMA,
        ],
        compiler_params=pltpu.CompilerParams(
            collective_id=collective_id, has_side_effects=True, vmem_limit_bytes=40 << 20
        ),
        name="spread_sequence",
    )(rows)


def fold_kernel(part_ref, out_ref, across, beside, summed, send_sem, recv_sem):
    tok = out_ref.shape[0]
    half = tok // 2
    z, core, y, x = place()
    me = y * 2 + x
    near = others()
    greet([(None, target) for target, _ in near[:2]])
    sends = Sends(send_sem, near[0][0])

    def rows(who, part):
        start = who * tok + part * half
        return part_ref.at[pl.ds(pl.multiple_of(start, half), half)]

    def landing(slot, part):
        return beside.at[slot, pl.ds(part * half, half)]

    for slot in range(2):
        sends.send(rows(near[2][1], slot), across.at[slot], recv_sem.at[0, slot], near[slot][0])
    for slot in range(2):
        sends.send(
            rows(near[slot][1], slot), landing(slot, slot), recv_sem.at[1, slot], near[slot][0]
        )
    for slot in range(2):
        part = 1 - slot
        sends.arrived(across.at[part], recv_sem.at[0, part])
        add_into(summed.at[slot], (rows(near[slot][1], part), across.at[part]), half)
        sends.send(summed.at[slot], landing(slot, part), recv_sem.at[2, slot], near[slot][0])
    for slot in range(2):
        sends.arrived(landing(slot, slot), recv_sem.at[1, slot])
        sends.arrived(landing(slot, 1 - slot), recv_sem.at[2, slot])
    own = part_ref.at[pl.ds(pl.multiple_of(me * tok, tok), tok)]
    add_into(out_ref, (own, beside.at[0], beside.at[1]), tok)
    sends.finish()


def fold_sequence(part, collective_id):
    total, width = part.shape
    tok = total // 4
    return pl.pallas_call(
        fold_kernel,
        out_shape=jax.ShapeDtypeStruct((tok, width), jnp.float32),
        in_specs=[pl.BlockSpec(memory_space=pltpu.VMEM)],
        out_specs=pl.BlockSpec(memory_space=pltpu.VMEM),
        scratch_shapes=[
            pltpu.VMEM((2, tok // 2, width), part.dtype),
            pltpu.VMEM((2, tok, width), part.dtype),
            pltpu.VMEM((2, tok // 2, width), part.dtype),
            pltpu.SemaphoreType.DMA((6,)),
            pltpu.SemaphoreType.DMA((3, 2)),
        ],
        compiler_params=pltpu.CompilerParams(
            collective_id=collective_id, has_side_effects=True, vmem_limit_bytes=40 << 20
        ),
        name="fold_sequence",
    )(part)


def weight_kernel(
    grad_ref,
    fold_ref,
    out_ref,
    fold_out,
    pair,
    part,
    landed,
    from_up,
    from_down,
    done,
    folds,
    send_sem,
    pair_sem,
    cross_sem,
    fold_sem,
    write_sem,
    *ladder_sems,
):
    depth = done.shape[1]
    half = depth // 2
    block = half // PER
    tok = fold_out.shape[0]
    z, core, y, x = place()
    me = y * 2 + x
    partner = device(z, 1 - core, y, x)
    up, down = device(z + 1, core, y, x), device(z - 1, core, y, x)
    near = [(device(z, core, y, x), me)] + others()
    greet(
        [(None, partner)]
        + [(None, target) for target, _ in near[1:]]
        + [(z < PLANES - 1, up), (z > 0, down)]
    )
    sends = Sends(send_sem, partner)

    def own_rows(n, which):
        start = pl.multiple_of(near[n][1] * depth + which * half, half)
        return grad_ref.at[pl.ds(start, half)]

    for n in range(4):
        sends.send(own_rows(n, 1 - core), pair.at[n], pair_sem.at[n], partner)
    for n in range(4):
        sends.arrived(pair.at[n], pair_sem.at[n])
        target = part.at[n - 1] if n else landed.at[0]
        add_into(target, (own_rows(n, core), pair.at[n]), half)
        if n:
            sends.send(target, landed.at[n], cross_sem.at[n - 1], near[n][0])
    for n in (1, 2, 3):
        target, who = near[n]
        rows = fold_ref.at[pl.ds(pl.multiple_of(who * tok, tok), tok)]
        sends.send(rows, folds.at[n - 1], fold_sem.at[n - 1], target)

    def before(n):
        @pl.when(jnp.logical_and(n % PER == 0, n > 0))
        def _():
            sends.arrived(landed.at[n // PER], cross_sem.at[n // PER - 1])

    def done_rows(n, which):
        source = n // PER
        who = ((y + source // 2) % 2) * 2 + (x + source % 2) % 2
        start = pl.multiple_of(which * half + (n % PER) * block, block)
        return done.at[who, pl.ds(start, block)]

    ladder_step, closed, close = ladder(
        sends,
        LADDER,
        before,
        lambda n: landed.at[n // PER, pl.ds(pl.multiple_of((n % PER) * block, block), block)],
        lambda n: from_up.at[n],
        lambda n: from_down.at[n],
        done_rows,
        block,
        ladder_sems,
    )

    @pl.loop(0, LADDER + LADDER_MORE)
    def _(m):
        ladder_step(m)

    for n in range(3):
        sends.arrived(folds.at[n], fold_sem.at[n])
    add_into(
        fold_out,
        [fold_ref.at[pl.ds(pl.multiple_of(me * tok, tok), tok)]] + [folds.at[n] for n in range(3)],
        tok,
    )
    single = HEAD_SIZE
    heads = QUERY_HEADS // 4 * HEAD_SIZE
    writes = []

    @pl.loop(0, LADDER)
    def _(n):
        closed(n)

    for n in range(4):
        who = near[n][1]
        for c, (base, width, offset) in enumerate(
            (
                (0, heads, 0),
                (QUERY_HEADS * HEAD_SIZE, single, heads),
                ((QUERY_HEADS + KEY_VALUE_HEADS) * HEAD_SIZE, single, heads + single),
            )
        ):
            copy = pltpu.make_async_copy(
                done.at[who, :, pl.ds(offset, width)],
                out_ref.at[:, pl.ds(pl.multiple_of(base + who * width, 128), width)],
                write_sem.at[n * 3 + c],
            )
            copy.start()
            writes.append(copy)
    close()
    for copy in writes:
        copy.wait()
    sends.finish()


def weight_reduce(grad, fold, collective_id):
    rows, columns = grad.shape
    depth = rows // 4
    half = depth // 2
    tok, width = fold.shape[0] // 4, fold.shape[1]
    dtype = grad.dtype
    return pl.pallas_call(
        weight_kernel,
        out_shape=[
            jax.ShapeDtypeStruct((depth, columns * 4), dtype),
            jax.ShapeDtypeStruct((tok, width), jnp.float32),
        ],
        in_specs=[pl.BlockSpec(memory_space=pltpu.VMEM)] * 2,
        out_specs=[pl.BlockSpec(memory_space=pltpu.HBM), pl.BlockSpec(memory_space=pltpu.VMEM)],
        scratch_shapes=[
            pltpu.VMEM((4, half, columns), dtype),
            pltpu.VMEM((3, half, columns), dtype),
            pltpu.VMEM((4, half, columns), dtype),
            pltpu.VMEM((LADDER, half // PER, columns), dtype),
            pltpu.VMEM((LADDER, half // PER, columns), dtype),
            pltpu.VMEM((4, depth, columns), dtype),
            pltpu.VMEM((3, tok, width), dtype),
            pltpu.SemaphoreType.DMA((10,)),
            pltpu.SemaphoreType.DMA((4,)),
            pltpu.SemaphoreType.DMA((3,)),
            pltpu.SemaphoreType.DMA((3,)),
            pltpu.SemaphoreType.DMA((12,)),
        ]
        + ladder_scratch(LADDER),
        compiler_params=pltpu.CompilerParams(
            collective_id=collective_id, has_side_effects=True, vmem_limit_bytes=56 << 20
        ),
        name="weight_reduce",
    )(grad, fold)


def project_back_kernel(
    grad_ref,
    weight_ref,
    normed_ref,
    x_ref,
    experts_ref,
    part_ref,
    grad_weight_ref,
    gain_ref,
    experts_out,
    inverse,
    ring,
    load_sem,
    store_sem,
):
    stripes = x_ref.shape[1] // 256
    chunk = ring.shape[1]
    slots = ring.shape[0]
    each = experts_ref.shape[2] // chunk
    chunks = 3 * each
    per = chunks // stripes

    def rows(ref, c):
        return ref.at[0, c // each, pl.ds(pl.multiple_of((c % each) * chunk, chunk), chunk)]

    def load(c):
        return pltpu.make_async_copy(
            rows(experts_ref, c), ring.at[c % slots], load_sem.at[c % slots]
        )

    def store(c):
        return pltpu.make_async_copy(
            ring.at[c % slots], rows(experts_out, c), store_sem.at[c % slots]
        )

    for c in range(slots):
        load(c).start()

    @pl.loop(0, x_ref.shape[0] // 64)
    def _(n):
        span = pl.ds(pl.multiple_of(n * 64, 64), 64)
        inverse[span] = inverse_rms(x_ref[span].astype(jnp.float32))

    @pl.loop(0, stripes)
    def _(i):
        for k in range(per):
            load(i * per + k).wait()
            store(i * per + k).start()
        span = pl.ds(pl.multiple_of(i * 256, 256), 256)
        part = mm(grad_ref[...], weight_ref[span], (1, 1))
        part_ref[:, span] = part.astype(jnp.bfloat16)
        scaled = part * x_ref[:, span].astype(jnp.float32) * inverse[...]
        gain_ref[:, span] = jnp.sum(scaled, axis=0, keepdims=True)
        grad_weight_ref[span] = mm(normed_ref[:, span], grad_ref[...], (0, 0)).astype(jnp.bfloat16)
        for k in range(per):
            store(i * per + k).wait()

            @pl.when(i * per + k + slots < chunks)
            def _():
                load(i * per + k + slots).start()


def project_back(grad, weight, normed, x, experts):
    seq, width = x.shape
    bf, f4 = jnp.bfloat16, jnp.float32
    return pl.pallas_call(
        project_back_kernel,
        out_shape=[
            jax.ShapeDtypeStruct((seq, width), bf),
            jax.ShapeDtypeStruct(weight.shape, bf),
            jax.ShapeDtypeStruct((1, width), f4),
            jax.ShapeDtypeStruct(experts.shape, f4),
        ],
        in_specs=[pl.BlockSpec(memory_space=pltpu.VMEM)] * 4
        + [pl.BlockSpec(memory_space=pltpu.HBM)],
        out_specs=[pl.BlockSpec(memory_space=pltpu.VMEM)] * 3
        + [pl.BlockSpec(memory_space=pltpu.HBM)],
        scratch_shapes=[
            pltpu.VMEM((seq, 1), f4),
            pltpu.VMEM((6, 256, experts.shape[3]), f4),
            pltpu.SemaphoreType.DMA((6,)),
            pltpu.SemaphoreType.DMA((6,)),
        ],
        compiler_params=pltpu.CompilerParams(vmem_limit_bytes=48 << 20),
        name="project_back",
    )(grad, weight, normed, x, experts)


def split_body(
    block_in,
    segments,
    routes,
    attn_gain,
    query_key_value_weight,
    q_gain,
    k_gain,
    w_out,
    ffn_gain,
    router,
    expert_weights,
    cotangent,
):
    tok, width = block_in.shape
    seq = segments.shape[0]
    experts = router.shape[1]
    capacity = tok * routes.shape[1] * 2 // experts
    heads = QUERY_HEADS // 4
    both = ("rep", "shard")
    upstream_all = lax.all_gather(cotangent, both, axis=0, tiled=True)
    x_all, weight = start_exchange(block_in, query_key_value_weight, 0)

    mask = jnp.any(
        routes[:, :, None] == jnp.arange(experts, dtype=jnp.int32)[None, None, :], axis=1
    )
    mask_f = mask.astype(jnp.float32)
    earlier = (jnp.arange(tok)[:, None] > jnp.arange(tok)[None, :]).astype(jnp.bfloat16)
    slot = jnp.dot(earlier, mask.astype(jnp.bfloat16), preferred_element_type=jnp.float32)
    slot_table = jnp.where(mask, slot, -4096.0).T

    cosine, sine = rope_tables(jnp.arange(seq, dtype=jnp.int32))
    cosine = cosine[:, 0]
    sine = sine[:, 0] * jnp.where(jnp.arange(HEAD_SIZE) < HEAD_SIZE // 2, -1.0, 1.0)
    normed_one, raw, q_rot, k_rot, values, attended, lse, partial = attend(
        x_all, weight, w_out, attn_gain, q_gain, k_gain, cosine, sine, segments
    )
    inputs = block_in.astype(jnp.float32)
    middle = inputs + fold_sequence(partial, 1)
    scale_two = rms_scale(middle)
    normed_two = (middle * scale_two * ffn_gain).astype(jnp.bfloat16)
    logits = jnp.dot(normed_two, router, preferred_element_type=jnp.float32)
    weights = jax.nn.softmax(logits, axis=-1)
    picked = weights * mask_f
    total = jnp.sum(picked, axis=1, keepdims=True)
    gates = picked / total
    table = jnp.concatenate([gates.T, slot_table], axis=0)
    tokens_all, _, out_part, grad_part, gate_part, rows_held, hidden_held = run_experts(
        normed_two, table, upstream_all, expert_weights, capacity, 2
    )
    grad_gates = lax.all_to_all(gate_part, both, split_axis=0, concat_axis=0, tiled=True).T
    grad_from_experts, grad_experts = reduce_all(grad_part, 3, expert=[rows_held, hidden_held])
    grad_from_experts = grad_from_experts.astype(jnp.float32)

    upstream = cotangent.astype(jnp.float32)
    grad_picked = grad_gates / total - jnp.sum(grad_gates * picked, axis=1, keepdims=True) / (
        total * total
    )
    grad_weights = grad_picked * mask_f
    grad_logits = weights * (grad_weights - jnp.sum(grad_weights * weights, axis=1, keepdims=True))
    grad_from_router = jnp.dot(
        grad_logits, router.astype(jnp.float32).T, precision=lax.Precision.HIGHEST
    )
    grad_norm_two, grad_ffn_gain = rms_back(
        middle, scale_two, ffn_gain, grad_from_experts + grad_from_router
    )
    grad_middle = upstream + grad_norm_two
    grad_middle_all = spread_sequence(grad_middle.astype(jnp.bfloat16), 5)
    grad_out = lax.dot_general(
        attended, grad_middle_all, (((0,), (0,)), ((), ())), preferred_element_type=jnp.float32
    ).astype(jnp.bfloat16)
    grad_attended = jnp.dot(
        grad_middle_all, w_out.T, preferred_element_type=jnp.float32
    ).astype(jnp.bfloat16)
    delta = attended.astype(jnp.float32) * grad_attended.astype(jnp.float32)
    delta = jnp.sum(delta.reshape(seq, heads, HEAD_SIZE), axis=2).T
    expert_sum, grad_out, grad_qkv_b, grad_gains = reduce_all(
        out_part,
        4,
        grad_out,
        [
            q_rot,
            k_rot,
            values,
            raw,
            grad_attended,
            lse,
            delta,
            q_gain[None],
            k_gain[None],
            cosine,
            sine,
            segments[:, None],
            segments[None],
        ],
    )
    block_out = (middle + expert_sum.astype(jnp.float32)).astype(jnp.bfloat16)
    grad_out = grad_out.astype(jnp.float32)
    grad_q_gain, grad_k_gain = grad_gains[0], grad_gains[1]
    norm_part, grad_weight, grad_attn_gain, grad_experts = project_back(
        grad_qkv_b, weight, normed_one, x_all, grad_experts
    )
    grad_attn_gain = grad_attn_gain[0]
    gains = jnp.concatenate([grad_attn_gain, grad_ffn_gain, grad_q_gain, grad_k_gain])
    lines = gains.shape[0] // tok
    spare = -(lines + experts) % 16
    small = jnp.concatenate(
        [grad_logits.T, gains.reshape(lines, tok), jnp.zeros((spare, tok), jnp.float32)], axis=0
    )
    small_all = lax.all_gather(small, both)
    grad_qkv, grad_norm_one = weight_reduce(grad_weight, norm_part, 7)
    grad_qkv = grad_qkv.astype(jnp.float32)
    grad_inputs, _ = rms_back(inputs, rms_scale(inputs), attn_gain, grad_norm_one)
    grad_input = (grad_middle + grad_inputs).astype(jnp.bfloat16)
    gains = jnp.sum(small_all[:, experts : experts + lines], axis=0).reshape(-1)
    grad_attn_gain, grad_ffn_gain, grad_q_gain, grad_k_gain = jnp.split(
        gains, (width, 2 * width, 2 * width + HEAD_SIZE)
    )
    logits_all = small_all[:, :experts].transpose(1, 0, 2).reshape(experts, -1)
    high = lax.reduce_precision(logits_all, 8, 7)
    middle_part = lax.reduce_precision(logits_all - high, 8, 7)
    low = logits_all - high - middle_part
    pieces = jnp.concatenate([high, middle_part, low], axis=0).astype(jnp.bfloat16)
    pieces = jnp.dot(pieces, tokens_all, preferred_element_type=jnp.float32)
    grad_router = jnp.sum(pieces.reshape(3, experts, width), axis=0).T
    return (
        block_out,
        grad_input,
        grad_attn_gain,
        grad_qkv,
        grad_q_gain,
        grad_k_gain,
        grad_out,
        grad_ffn_gain,
        grad_router,
        grad_experts,
    )


def solution(mesh):
    placed = (
        P(("rep", "shard"), None),
        P("rep"),
        P(("rep", "shard"), None),
        P(),
        P("shard", None),
        P(),
        P(),
        P("shard", None),
        P(),
        P(),
        P(("rep", "shard"), None, None, None),
        P(("rep", "shard"), None),
    )
    body = split_body if dict(mesh.shape) == {"rep": 8, "shard": 4} else plain_body
    return jax.shard_map(
        body,
        mesh=mesh,
        in_specs=placed,
        out_specs=(
            P(("rep", "shard"), None),
            P(("rep", "shard"), None),
            P(),
            P("shard", None),
            P(),
            P(),
            P("shard", None),
            P(),
            P(),
            P(("rep", "shard"), None, None, None),
        ),
        check_vma=False,
    )
```

profile of v0, /device:TPU:0, one launch (start us, length us, event | category | flops | bytes accessed | tf_op | source)
XLA Modules:
  0.0 672.2 jit_solution(14545825167893033250)
XLA Ops:
  7.2 0.7 all-gather.4.cloned.1.call-update
  7.9 1.5 copy.36.seg_col.refs_13_
  9.5 1.0 copy-done.4
  10.5 2.5 copy-done.6
  13.0 74.9 %start_exchange.1 = (bf16[512,2048]{1,0:T(8,128)(2,1)S(1)}, bf16[2048,1280]{1,0:T(8,128)(2,1)S(1)}) custom-call(bf16[128,2048]{1,0:T(8,128)(2,1)S(1)} %copy-done.4, bf16[512,5120]{1,0:T(8,128)(2,1)S(1)} %copy-done.6), custom_call_target="tpu_custom_call" | custom-call | tf_op jit(solution)/shard_map/start_exchange/pallas_call | solution.py:1541
  87.9 2.3 copy-done.2
  90.2 1.5 copy-done.3
  91.7 1.0 multiply_sine_fusion
  92.7 1.0 pad_maximum_fusion
  93.7 26.5 %attend.1 = (bf16[512,2048]{1,0:T(8,128)(2,1)}, f32[512,1280]{1,0:T(8,128)}, bf16[512,1024]{1,0:T(8,128)(2,1)}, bf16[512,128]{1,0:T(8,128)(2,1)}, bf16[512,128]{...) custom-call(bf16[512,2048]{1,0:T(8,128)(2,1)} %copy-done.3, ...), custom_call_target="tpu_custom_call" | custom-call | tf_op jit(solution)/shard_map/attend/pallas_call | solution.py:881
  120.3 1.6 copy-done.9
  121.9 20.8 %fold_sequence.1 = f32[128,2048]{1,0:T(8,128)S(1)} custom-call(bf16[512,2048]{1,0:T(8,128)(2,1)S(1)} %copy-done.9), custom_call_target="tpu_custom_call" | custom-call | tf_op jit(solution)/shard_map/fold_sequence/pallas_call | solution.py:1660
  142.8 0.2 multiply_reduce_fusion.2
  143.0 1.0 copy-done.11
  144.2 0.8 copy-done.14
  144.9 0.3 fusion.25
  145.5 0.6 pad_maximum_fusion.1.table_ref
  146.1 121.4 %run_experts.1 = (bf16[4096,2048]{1,0:T(8,128)(2,1)}, f32[2048,128]{1,0:T(8,128)}, bf16[4096,2048]{1,0:T(8,128)(2,1)}, bf16[4096,2048]{1,0:T(8,128)(2,1)}, f32[3...) custom-call(bf16[128,2048]{1,0:T(8,128)(2,1)} %copy-done.14, ...), custom_call_target="tpu_custom_call" | custom-call | tf_op jit(solution)/shard_map/run_experts/pallas_call | solution.py:731
  267.6 4.9 all-to-all-start
  272.6 90.0 %reduce_all.2 = (bf16[128,2048]{1,0:T(8,128)(2,1)}, f32[1,3,2048,768]{3,2,1,0:T(8,128)}) custom-call(bf16[4096,2048]{1,0:T(8,128)(2,1)} %get-tuple-element.43.refs_0_, bf16[2,2048,2048]{2,1,0:T(8,128)(2,1)} %get-tuple-element.44.refs_1_, bf16[3,2048,768]{2,1,0:T(8,128)(2,1)} %get-tuple-element.45.refs_2_), custom_call_target="tpu_custom_call" | custom-call | tf_op jit(solution)/shard_map/reduce_all/pallas_call | solution.py:1419
  362.8 2.4 multiply_reduce_fusion
  365.2 1.5 fusion.24
  366.7 18.6 %spread_sequence.1 = bf16[512,2048]{1,0:T(8,128)(2,1)S(1)} custom-call(bf16[128,2048]{1,0:T(8,128)(2,1)S(1)} %get-tuple-element.70.x_ref), custom_call_target="tpu_custom_call" | custom-call | tf_op jit(solution)/shard_map/spread_sequence/pallas_call | solution.py:1605
  385.3 2.4 convolution_convert_fusion.1.refs_6_
  387.6 4.4 convolution_convert_fusion.refs_1_
  392.0 0.4 multiply_bitcast_fusion
  392.4 0.5 copy.42
  392.9 0.6 reduce_sum.114
  393.5 0.7 copy.38
  394.2 120.8 %reduce_all.3 = (bf16[128,2048]{1,0:T(8,128)(2,1)}, bf16[1024,2048]{1,0:T(8,128)(2,1)}, bf16[512,1280]{1,0:T(8,128)(2,1)}, f32[8,128]{1,0:T(8,128)}) custom-call(bf16[4096,2048]{1,0:T(8,128)(2,1)} %get-tuple-element.41.refs_0_, bf16[1024,2048]{1,0:T(8,128)(2,1)} %convolution_convert_fusion.refs_1_, bf16[512,1024]{1,0:T(8,128)(2,1)} %get-tuple-element.48.refs_2_, ...), custom_call_target="tpu_custom_call" | custom-call | tf_op jit(solution)/shard_map/reduce_all/pallas_call | solution.py:1419
  515.0 0.8 slice_bitcast_fusion.6
  515.8 1.6 copy-done.7
  517.4 1.3 copy-done.10
  518.7 20.1 %project_back.1 = (bf16[512,2048]{1,0:T(8,128)(2,1)S(1)}, bf16[2048,1280]{1,0:T(8,128)(2,1)}, f32[1,2048]{1,0:T(1,128)S(1)}, f32[1,3,2048,768]{3,2,1,0:T(8,128)}) custom-call(bf16[512,1280]{1,0:T(8,128)(2,1)S(1)} %copy-done.10, bf16[2048,1280]{1,0:T(8,128)(2,1)} %copy-done.2, bf16[512,2048]{1,0:T(8,128)(2,1)S(1)} %copy-done.7, bf16[512,2048]{1,0:T(8,128)(2,1)} %copy-done.3, ...), custom_call_target="tpu_custom_call" | custom-call | tf_op jit(solution)/shard_map/project_back/pallas_call | solution.py:1896
  538.8 1.3 copy-done.8
  540.1 0.7 maximum_maximum_fusion
  540.9 96.3 %weight_reduce.1 = (bf16[512,5120]{1,0:T(8,128)(2,1)}, f32[128,2048]{1,0:T(8,128)}) custom-call(bf16[2048,1280]{1,0:T(8,128)(2,1)} %get-tuple-element.57.grad_ref, bf16[512,2048]{1,0:T(8,128)(2,1)} %copy-done.8), custom_call_target="tpu_custom_call" | custom-call | tf_op jit(solution)/shard_map/weight_reduce/pallas_call | solution.py:1801
  637.2 8.1 %convert_element_type.87 = f32[512,5120]{1,0:T(8,128)} convert(bf16[512,5120]{1,0:T(8,128)(2,1)} %get-tuple-element.62) | non-fusion elementwise | flops 2621440 | bytes 15728640 | tf_op jit(solution)/shard_map/convert_element_type | solution.py:2030
  645.3 4.4 convert_element_type.88
  649.7 0.3 fusion
  650.1 0.9 add_convert_fusion
  651.0 1.3 fusion.4
  652.3 1.1 slice_reduce_fusion
  653.4 0.6 slice_bitcast_fusion.1
  654.0 0.5 slice_bitcast_fusion.3
  654.5 1.2 reduce-precision_convert_fusion.1
  655.7 8.6 %fusion.6 = f32[96,2048]{1,0:T(8,128)S(1)} fusion(bf16[4096,2048]{1,0:T(8,128)(2,1)} %get-tuple-element.64, bf16[32,4096]{1,0:T(8,128)(2,1)S(1)} %get-tuple-element.75, bf16[32,4096]{1,0:T(8,128)(2,1)S(1)} %get-tuple-element.76, bf16[32,4096]{1,0:T(8,128)(2,1)S(1)} %get-tuple-element.74), kind=kOutput, calls=%fused_computation.21 | convolution fusion | flops 1612972032 | bytes 18350080 | tf_op jit(solution)/shard_map/dot_general | solution.py:2042
  664.3 0.7 reduce_sum.119
  (68 shorter events, 0.8 us)
Async XLA Ops:
  7.2 137.8 %copy-start = (bf16[2048,32]{0,1:T(8,128)(2,1)S(1)}, bf16[2048,32]{0,1:T(8,128)(2,1)}, u32[]{:S(2)}) copy-start(bf16[2048,32]{0,1:T(8,128)(2,1)} %param.21) | copy-start | bytes 393220
  7.2 138.9 %all-gather.4.cloned.1.call-start = ((), (), s32[]{:S(2)}) async-start(), calls=%async_computation.1 | async-start | bytes 17301504 | tf_op jit(solution)/shard_map/all_gather | solution.py:1939
  9.5 1.0 copy-start.4
  10.5 2.5 copy-start.6
  87.9 2.4 copy-start.2
  90.2 1.5 copy-start.3
  120.3 22.5 %copy-start.5 = (bf16[128,2048]{1,0:T(8,128)(2,1)S(1)}, bf16[128,2048]{1,0:T(8,128)(2,1)}, u32[]{:S(2)}) copy-start(bf16[128,2048]{1,0:T(8,128)(2,1)} %x_ref.1) | copy-start | bytes 1572868
  120.3 1.6 copy-start.9
  121.9 22.1 %copy-start.23 = (f32[2048]{0:T(1024)S(1)}, f32[2048]{0:T(1024)}, u32[]{:S(2)}) copy-start(f32[2048]{0:T(1024)} %param.20) | copy-start | bytes 24580
  142.7 2.5 copy-start.25
  143.0 1.0 copy-start.11
  144.1 0.8 copy-start.14
  267.6 95.1 %all-to-all-start = ((f32[32,1,128]{2,1,0:T(1,128)}), f32[32,1,128]{2,1,0:T(1,128)S(1)}, u32[]{:S(2)}, u32[]{:S(2)}) async-start(f32[32,1,128]{2,1,0:T(1,128)} %bitcast.79), calls=%async_computation | async-start | bytes 32768 | tf_op jit(solution)/shard_map/all_to_all | solution.py:1969
  272.5 379.8 %all-gather.6.cloned.1.call-start = ((), (), s32[]{:S(2)}) async-start(), calls=%async_computation.2 | async-start | bytes 1351680 | tf_op jit(solution)/shard_map/all_gather | solution.py:2028
  362.6 2.5 copy-start.12
  362.7 2.5 copy-start.20
  365.2 20.0 %copy-start.15 = (bf16[1024,2048]{1,0:T(8,128)(2,1)S(1)}, bf16[1024,2048]{1,0:T(8,128)(2,1)}, u32[]{:S(2)}) copy-start(bf16[1024,2048]{1,0:T(8,128)(2,1)} %w_out_ref.1) | copy-start | bytes 12582916
  385.2 2.4 copy-start.21
  387.6 4.4 copy-start.19
  515.8 1.6 copy-start.7
  517.4 1.3 copy-start.10
  538.8 1.3 copy-start.8
  637.2 8.1 %copy-start.16 = (bf16[1024,2048]{1,0:T(8,128)(2,1)S(1)}, bf16[1024,2048]{1,0:T(8,128)(2,1)}, u32[]{:S(2)}) copy-start(bf16[1024,2048]{1,0:T(8,128)(2,1)} %get-tuple-element.63) | copy-start | bytes 12582916
  645.2 4.5 copy-start.18
  645.2 4.5 copy-start.24
  645.2 4.8 copy-start.13
  645.3 4.8 copy-start.22
  649.7 1.3 copy-start.17
  655.7 9.3 %copy-start.1 = (bf16[2048,32]{0,1:T(8,128)(2,1)S(1)}, bf16[2048,32]{0,1:T(8,128)(2,1)}, u32[]{:S(2)}) copy-start(bf16[2048,32]{0,1:T(8,128)(2,1)} %param.21) | copy-start | bytes 393220
Sparse Core Ops, SparseCore 0:
  10.9 135.1 all-gather.3
  541.0 73.4 all-gather.5
where the time goes:
time: 677 us; the launch traced here: 672 us
  Pallas kernels  589 us (87%)
  other arithmetic  24.4 us (4%)
  local copies, waits for them, and re-layouts  19.7 us (3%)
  matrix products  18.2 us (3%)
  between operations  14.7 us (2%)
    pallas_call x2, Pallas kernels, reduce_all(): pl.pallas_call(functools.partial(reduce_kernel, weight is not None), out_...  211 us
    pallas_call x1, Pallas kernels, run_experts(): pl.pallas_call(experts_kernel, out_shape=[jax.ShapeDtypeStruct((total, wi...  121 us
    pallas_call x1, Pallas kernels, weight_reduce(): pl.pallas_call(weight_kernel, out_shape=[jax.ShapeDtypeStruct((depth, col...  96.3 us
    pallas_call x1, Pallas kernels, start_exchange(): pl.pallas_call(start_kernel, out_shape=[jax.ShapeDtypeStruct((tok * 4, wi...  74.9 us
    pallas_call x1, Pallas kernels, attend(): pl.pallas_call(attend_kernel, out_shape=[out((seq, width), bf), out((seq,...  26.5 us
    pallas_call x1, Pallas kernels, fold_sequence(): pl.pallas_call(fold_kernel, out_shape=jax.ShapeDtypeStruct((tok, width),...  20.8 us
    pallas_call x1, Pallas kernels, project_back(): pl.pallas_call(project_back_kernel, out_shape=[jax.ShapeDtypeStruct((seq,...  20.1 us
    pallas_call x1, Pallas kernels, spread_sequence(): pl.pallas_call(spread_kernel, out_shape=jax.ShapeDtypeStruct((tok * 4, wi...  18.6 us
  transfers between devices with their start and end apart: 3, of which 0 were waited for; matrix products, arithmetic and copies ran while one was open for 3% of the time, Pallas kernels for 46%

commit v1 on v0

--- a/solution.py
+++ b/solution.py
@@ -910,9 +910,9 @@
 
 
 def backward_steps(refs):
-    q_ref, k_ref, v_ref, raw_ref, upstream, lse_ref, delta_ref = refs[:7]
-    q_gain_ref, k_gain_ref, cos_ref, sin_ref, seg_col, seg_row = refs[7:13]
-    grad_ref, gains_ref, bias, grad_k, grad_v = refs[13:]
+    q_ref, k_ref, v_ref, raw_ref, upstream, lse_ref = refs[:6]
+    q_gain_ref, k_gain_ref, cos_ref, sin_ref, seg_col, seg_row = refs[6:12]
+    grad_ref, gains_ref, bias, grad_k, grad_v = refs[12:]
     seq, size = k_ref.shape
     heads = q_ref.shape[1] // size
     scale = size ** (-0.5)
@@ -935,15 +935,15 @@
         gains_ref[line : line + 1] += jnp.sum(turned * raw * inverse, axis=0, keepdims=True)
 
     def head(h):
-        columns = pl.ds(h * size, size)
+        columns = pl.ds(pl.multiple_of(h * size, size), size)
         for first, keys in ((0, half), (half, seq)):
             queries = pl.ds(first, half)
             q, above = q_ref[queries, columns], upstream[queries, columns]
             score = mm(k_ref[:keys], q, (1, 1)) * scale + bias[:keys, first : first + half]
-            probs = jnp.exp(score - lse_ref[h : h + 1, first : first + half])
+            probs = jnp.exp(score - lse_ref[pl.ds(h, 1), queries])
             grad_v[:keys] += mm(probs.astype(jnp.bfloat16), above, (1, 0))
             grad_p = mm(v_ref[:keys], above, (1, 1))
-            delta = delta_ref[h : h + 1, first : first + half]
+            delta = jnp.sum(probs * grad_p, axis=0, keepdims=True)
             grad_score = (probs * (grad_p - delta) * scale).astype(jnp.bfloat16)
             grad_k[:keys] += mm(grad_score, q, (1, 0))
             grad_q = mm(grad_score, k_ref[:keys], (0, 0))
@@ -955,7 +955,7 @@
             turn_back(grad_k[queries], queries, pl.ds(heads * size, size), k_gain_ref[...], 1)
         grad_ref[:, (heads + 1) * size :] = grad_v[...].astype(jnp.bfloat16)
 
-    return [prepare] + [functools.partial(head, h) for h in range(heads)] + [keys_and_values]
+    return prepare, head, keys_and_values
 
 
 class Sends:
@@ -1109,14 +1109,15 @@
     refs = list(refs)
     part_ref = refs.pop(0)
     weight_ref = refs.pop(0) if with_weight else None
-    back = [refs.pop(0) for _ in range(13)] if with_weight else []
+    back = [refs.pop(0) for _ in range(12)] if with_weight else []
     rows_ref, hidden_ref = (None, None) if with_weight else (refs.pop(0), refs.pop(0))
     out_ref = refs.pop(0)
     weight_out = refs.pop(0) if with_weight else None
     grad_w = None if with_weight else refs.pop(0)
     back += [refs.pop(0) for _ in range(2)] if with_weight else []
     kept, paired, x_half, x_full, y_half, y_full, from_up, from_down = refs[:8]
-    send_sem, pair_sem, x_sem, y_sem, z_sem, load_sem = refs[8:14]
+    send_sem, pair_sem, x_sem, y_sem, z_sem, load_sem, step_sem = refs[8:15]
+    refs = refs[:8] + refs[9:]
     rows = out_ref.shape[0]
     half = rows // 2
     z, core, y, x = place()
@@ -1138,6 +1139,10 @@
         sum((z == level).astype(jnp.int32) * tables[level][n] for level in range(PLANES))
         for n in range(PLANES)
     ]
+
+    def plane_at(n):
+        return sum((n == k).astype(jnp.int32) * order[k] for k in range(PLANES))
+
     spots = ((1 - y, 1 - x), (y, 1 - x), (1 - y, x), (y, x))
 
     def slot(plane, spot):
@@ -1202,7 +1207,7 @@
         held = rows_hold.shape[2]
 
         def fetch(i):
-            span = pl.ds(i * held, held)
+            span = pl.ds(pl.multiple_of(i * held, held), held)
             return (
                 pltpu.make_async_copy(
                     rows_ref.at[:, span], rows_hold.at[i % 2], part_sem.at[0, i % 2]
@@ -1216,24 +1221,25 @@
         for copy in fetch(0):
             copy.start()
 
+        sums[...] = jnp.zeros_like(sums)
+
         def add_product(i):
-            if i + 1 < parts:
+            @pl.when(i + 1 < parts)
+            def _():
                 for copy in fetch(i + 1):
                     copy.start()
+
             for copy in fetch(i):
                 copy.wait()
-            for matrix, source in ((0, 0), (1, 0), (2, 1)):
-
-                @pl.loop(0, sums.shape[1] // 512)
-                def _(n):
-                    span = pl.ds(pl.multiple_of(n * 512, 512), 512)
-                    product = mm(
-                        rows_hold[i % 2, source, :, span], hidden_hold[i % 2, matrix], (0, 0)
-                    )
-                    if i:
-                        sums[matrix, span] += product
-                    else:
-                        sums[matrix, span] = product
+            stripes = sums.shape[1] // 512
+
+            @pl.loop(0, 3 * stripes)
+            def _(n):
+                matrix = n // stripes
+                span = pl.ds(pl.multiple_of((n % stripes) * 512, 512), 512)
+                sums[matrix, span] += mm(
+                    rows_hold[i % 2, matrix // 2, :, span], hidden_hold[i % 2, matrix], (0, 0)
+                )
 
         write_sums = pltpu.make_async_copy(sums, grad_w.at[0], sum_sem)
 
@@ -1243,37 +1249,74 @@
         sends.arrived(paired.at[where], pair_sem.at[where])
         add_rows(kept.at[where], (paired.at[where],) + tuple(more), rows)
 
+    def across_copies(plane):
+        source = kept.at[slot(plane, 0)]
+        return (
+            remote(
+                source.at[pl.ds(0, half)],
+                x_half.at[plane],
+                step_sem.at[0, plane],
+                x_sem.at[plane],
+                x_next,
+            ),
+            remote(
+                source.at[pl.ds(half, half)],
+                y_half.at[plane],
+                step_sem.at[1, plane],
+                y_sem.at[plane],
+                y_next,
+            ),
+        )
+
+    def beside_copies(plane):
+        return (
+            remote(
+                kept.at[slot(plane, 1)],
+                x_full.at[plane],
+                step_sem.at[2, plane],
+                x_sem.at[4 + plane],
+                x_next,
+            ),
+            remote(
+                kept.at[slot(plane, 2)],
+                y_full.at[plane],
+                step_sem.at[3, plane],
+                y_sem.at[4 + plane],
+                y_next,
+            ),
+        )
+
     def across(plane):
         joined(plane, 0)
-        source = kept.at[slot(plane, 0)]
-        sends.send(source.at[pl.ds(0, half)], x_half.at[plane], x_sem.at[plane], x_next)
-        sends.send(source.at[pl.ds(half, half)], y_half.at[plane], y_sem.at[plane], y_next)
+        for copy in across_copies(plane):
+            copy.start()
 
     def beside(plane):
+        along_x, along_y = beside_copies(plane)
         joined(plane, 1)
         sends.arrived(y_half.at[plane], y_sem.at[plane])
         add_rows(kept.at[slot(plane, 1)].at[pl.ds(half, half)], (y_half.at[plane],), half)
-        sends.send(kept.at[slot(plane, 1)], x_full.at[plane], x_sem.at[4 + plane], x_next)
+        along_x.start()
         joined(plane, 2)
         sends.arrived(x_half.at[plane], x_sem.at[plane])
         add_rows(kept.at[slot(plane, 2)].at[pl.ds(0, half)], (x_half.at[plane],), half)
-        sends.send(kept.at[slot(plane, 2)], y_full.at[plane], y_sem.at[4 + plane], y_next)
+        along_y.start()
 
     def along(plane):
         sends.arrived(x_full.at[plane], x_sem.at[4 + plane])
         sends.arrived(y_full.at[plane], y_sem.at[4 + plane])
         joined(plane, 3, (x_full.at[plane], y_full.at[plane]))
 
-    moves = {}
-
-    def pass_on(n, first):
-        plane = order[n]
+    def onward(plane):
         total = kept.at[slot(plane, 3)]
-        if first:
-            fall = sends.make(total, from_up.at[plane], z_sem.at[0, plane], down, z > plane)
-            rise = sends.make(total, from_down.at[plane], z_sem.at[1, plane], up, z < plane)
-            moves[n] = (fall, rise)
-        fall, rise = moves[n]
+        return (
+            remote(total, from_up.at[plane], step_sem.at[4, plane], z_sem.at[0, plane], down),
+            remote(total, from_down.at[plane], step_sem.at[4, plane], z_sem.at[1, plane], up),
+        )
+
+    def pass_on(plane, first):
+        total = kept.at[slot(plane, 3)]
+        fall, rise = onward(plane)
         for copy, way, end, landing, sem in (
             (fall, z > plane, z == PLANES - 1, from_up.at[plane], z_sem.at[0, plane]),
             (rise, z < plane, z == 0, from_down.at[plane], z_sem.at[1, plane]),
@@ -1288,35 +1331,44 @@
                     add_rows(total, (landing,), rows)
                     copy.start()
 
-    total_steps = LADDER + LADDER_MORE
-    done_steps = 0
     if with_weight:
         fill[0]()
+        share = (LADDER + LADDER_MORE) // (2 * PLANES)
     for late, run in enumerate((across, beside)):
-        for n, plane in enumerate(order):
-            run(plane)
-            if not with_weight:
+
+        @pl.loop(0, PLANES)
+        def _(n):
+            run(plane_at(n))
+            if with_weight:
+                if not late:
+                    fill[1](n)
+                first = (late * PLANES + n) * share
+
+                @pl.loop(0, share)
+                def _(m):
+                    ladder_step(first + m)
+            else:
                 add_product(late * PLANES + n)
-            if with_weight:
-                if run is across:
-                    fill[1 + n]()
-                more = min(-(-total_steps // (2 * PLANES)), total_steps - done_steps)
-
-                @pl.loop(done_steps, done_steps + more)
-                def _(m):
-                    ladder_step(m)
-
-                done_steps += more
+
     if not with_weight:
         write_sums.start()
-    for n in range(PLANES):
-        along(order[n])
-        if n < PLANES - 1:
-            pass_on(n, True)
-        if n:
-            pass_on(n - 1, False)
+
+    @pl.loop(0, PLANES)
+    def _(n):
+        plane = plane_at(n)
+        along(plane)
+
+        @pl.when(n < PLANES - 1)
+        def _():
+            pass_on(plane, True)
+
+        @pl.when(n > 0)
+        def _():
+            pass_on(plane_at(n - 1), False)
+
         if with_weight:
-            fill[1 + PLANES + n]()
+            fill[1](PLANES + n)
+
     if with_weight:
         fill[-1]()
     mine = kept.at[slot(z, 3)]
@@ -1344,6 +1396,13 @@
         write.wait()
     else:
         write_sums.wait()
+
+    @pl.loop(0, PLANES)
+    def _(plane):
+        for copy in across_copies(plane) + beside_copies(plane):
+            copy.wait_send()
+        pl.when(plane != z)(onward(plane)[0].wait_send)
+
     sends.finish()
 
 
@@ -1364,12 +1423,13 @@
         pltpu.VMEM((4, rows, width), dtype),
         pltpu.VMEM((4, rows, width), dtype),
         pltpu.VMEM((4, rows, width), dtype),
-        pltpu.SemaphoreType.DMA((52,)),
+        pltpu.SemaphoreType.DMA((20,)),
         pltpu.SemaphoreType.DMA((16,)),
         pltpu.SemaphoreType.DMA((8,)),
         pltpu.SemaphoreType.DMA((8,)),
         pltpu.SemaphoreType.DMA((2, 4)),
         pltpu.SemaphoreType.DMA((16,)),
+        pltpu.SemaphoreType.DMA((5, 4)),
     ]
     operands = [part]
     if weight is not None:
@@ -1990,8 +2050,6 @@
     grad_attended = jnp.dot(
         grad_middle_all, w_out.T, preferred_element_type=jnp.float32
     ).astype(jnp.bfloat16)
-    delta = attended.astype(jnp.float32) * grad_attended.astype(jnp.float32)
-    delta = jnp.sum(delta.reshape(seq, heads, HEAD_SIZE), axis=2).T
     expert_sum, grad_out, grad_qkv_b, grad_gains = reduce_all(
         out_part,
         4,
@@ -2003,7 +2061,6 @@
             raw,
             grad_attended,
             lse,
-            delta,
             q_gain[None],
             k_gain[None],
             cosine,

time: 677 us -> 671 us (level)
    unnamed x53 -> x46, local copies, waits for them, and re-layouts: 15.5 us -> 15 us
where the time goes in v1:
time: 671 us; the launch traced here: 670 us
  Pallas kernels  588 us (88%)
  other arithmetic  24.8 us (4%)
  matrix products  19.2 us (3%)
  local copies, waits for them, and re-layouts  18.5 us (3%)
  between operations  14.4 us (2%)
    pallas_call x2, Pallas kernels, reduce_all(): pl.pallas_call(functools.partial(reduce_kernel, weight is not None), out_...  209 us
    pallas_call x1, Pallas kernels, run_experts(): pl.pallas_call(experts_kernel, out_shape=[jax.ShapeDtypeStruct((total, wi...  121 us
    pallas_call x1, Pallas kernels, weight_reduce(): pl.pallas_call(weight_kernel, out_shape=[jax.ShapeDtypeStruct((depth, col...  96.9 us
    pallas_call x1, Pallas kernels, start_exchange(): pl.pallas_call(start_kernel, out_shape=[jax.ShapeDtypeStruct((tok * 4, wi...  74.9 us
    pallas_call x1, Pallas kernels, attend(): pl.pallas_call(attend_kernel, out_shape=[out((seq, width), bf), out((seq,...  26.6 us
    pallas_call x1, Pallas kernels, fold_sequence(): pl.pallas_call(fold_kernel, out_shape=jax.ShapeDtypeStruct((tok, width),...  20.9 us
    pallas_call x1, Pallas kernels, project_back(): pl.pallas_call(project_back_kernel, out_shape=[jax.ShapeDtypeStruct((seq,...  20.1 us
    pallas_call x1, Pallas kernels, spread_sequence(): pl.pallas_call(spread_kernel, out_shape=jax.ShapeDtypeStruct((tok * 4, wi...  17.7 us
  transfers between devices with their start and end apart: 3, of which 0 were waited for; matrix products, arithmetic and copies ran while one was open for 3% of the time, Pallas kernels for 46%

profile of v1, /device:TPU:0, one launch (start us, length us, event | category | flops | bytes accessed | tf_op | source)
XLA Modules:
  0.0 670.1 jit_solution(10718574566755516314)
XLA Ops:
  7.2 0.7 all-gather.4.cloned.1.call-update
  7.9 1.5 copy.35.seg_col.refs_12_
  9.5 1.0 copy-done.4
  10.5 2.5 copy-done.6
  13.0 74.9 %start_exchange.1 = (bf16[512,2048]{1,0:T(8,128)(2,1)S(1)}, bf16[2048,1280]{1,0:T(8,128)(2,1)S(1)}) custom-call(bf16[128,2048]{1,0:T(8,128)(2,1)S(1)} %copy-done.4, bf16[512,5120]{1,0:T(8,128)(2,1)S(1)} %copy-done.6), custom_call_target="tpu_custom_call" | custom-call | tf_op jit(solution)/shard_map/start_exchange/pallas_call | solution.py:1601
  87.9 2.3 copy-done.2
  90.2 1.5 copy-done.3
  91.7 1.0 multiply_sine_fusion
  92.7 1.0 pad_maximum_fusion
  93.7 26.6 %attend.1 = (bf16[512,2048]{1,0:T(8,128)(2,1)}, f32[512,1280]{1,0:T(8,128)}, bf16[512,1024]{1,0:T(8,128)(2,1)}, bf16[512,128]{1,0:T(8,128)(2,1)}, bf16[512,128]{...) custom-call(bf16[512,2048]{1,0:T(8,128)(2,1)} %copy-done.3, ...), custom_call_target="tpu_custom_call" | custom-call | tf_op jit(solution)/shard_map/attend/pallas_call | solution.py:881
  120.3 1.6 copy-done.9
  121.9 20.9 %fold_sequence.1 = f32[128,2048]{1,0:T(8,128)S(1)} custom-call(bf16[512,2048]{1,0:T(8,128)(2,1)S(1)} %copy-done.9), custom_call_target="tpu_custom_call" | custom-call | tf_op jit(solution)/shard_map/fold_sequence/pallas_call | solution.py:1720
  142.8 0.2 multiply_reduce_fusion.2
  143.0 1.0 copy-done.11
  144.0 0.2 multiply_convert_fusion.x_ref
  144.1 0.8 copy-done.13
  144.9 0.3 fusion.25
  145.3 0.1 convolution_select_fusion
  145.5 0.6 pad_maximum_fusion.1.table_ref
  146.1 121.4 %run_experts.1 = (bf16[4096,2048]{1,0:T(8,128)(2,1)}, f32[2048,128]{1,0:T(8,128)}, bf16[4096,2048]{1,0:T(8,128)(2,1)}, bf16[4096,2048]{1,0:T(8,128)(2,1)}, f32[3...) custom-call(bf16[128,2048]{1,0:T(8,128)(2,1)} %copy-done.13, ...), custom_call_target="tpu_custom_call" | custom-call | tf_op jit(solution)/shard_map/run_experts/pallas_call | solution.py:731
  267.6 4.8 all-to-all-start
  272.4 0.0 all-gather.6.cloned.1.call-start
  272.5 0.1 pad.5.clone
  272.5 90.3 %reduce_all.2 = (bf16[128,2048]{1,0:T(8,128)(2,1)}, f32[1,3,2048,768]{3,2,1,0:T(8,128)}) custom-call(bf16[4096,2048]{1,0:T(8,128)(2,1)} %get-tuple-element.43.refs_0_, bf16[2,2048,2048]{2,1,0:T(8,128)(2,1)} %get-tuple-element.44.refs_1_, bf16[3,2048,768]{2,1,0:T(8,128)(2,1)} %get-tuple-element.45.refs_2_), custom_call_target="tpu_custom_call" | custom-call | tf_op jit(solution)/shard_map/reduce_all/pallas_call | solution.py:1479
  362.9 2.4 multiply_reduce_fusion
  365.4 2.8 fusion.24
  368.2 17.7 %spread_sequence.1 = bf16[512,2048]{1,0:T(8,128)(2,1)S(1)} custom-call(bf16[128,2048]{1,0:T(8,128)(2,1)S(1)} %get-tuple-element.70.x_ref), custom_call_target="tpu_custom_call" | custom-call | tf_op jit(solution)/shard_map/spread_sequence/pallas_call | solution.py:1665
  385.9 3.4 convolution_convert_fusion.1.refs_6_
  389.2 4.4 convolution_convert_fusion.refs_1_
  393.6 119.0 %reduce_all.3 = (bf16[128,2048]{1,0:T(8,128)(2,1)}, bf16[1024,2048]{1,0:T(8,128)(2,1)}, bf16[512,1280]{1,0:T(8,128)(2,1)}, f32[8,128]{1,0:T(8,128)}) custom-call(bf16[4096,2048]{1,0:T(8,128)(2,1)} %get-tuple-element.41.refs_0_, bf16[1024,2048]{1,0:T(8,128)(2,1)} %convolution_convert_fusion.refs_1_, bf16[512,1024]{1,0:T(8,128)(2,1)} %get-tuple-element.48.refs_2_, ...), custom_call_target="tpu_custom_call" | custom-call | tf_op jit(solution)/shard_map/reduce_all/pallas_call | solution.py:1479
  512.6 0.8 slice_bitcast_fusion.6
  513.4 1.6 copy-done.7
  515.0 1.3 copy-done.10
  516.3 20.1 %project_back.1 = (bf16[512,2048]{1,0:T(8,128)(2,1)S(1)}, bf16[2048,1280]{1,0:T(8,128)(2,1)}, f32[1,2048]{1,0:T(1,128)S(1)}, f32[1,3,2048,768]{3,2,1,0:T(8,128)}) custom-call(bf16[512,1280]{1,0:T(8,128)(2,1)S(1)} %copy-done.10, bf16[2048,1280]{1,0:T(8,128)(2,1)} %copy-done.2, bf16[512,2048]{1,0:T(8,128)(2,1)S(1)} %copy-done.7, bf16[512,2048]{1,0:T(8,128)(2,1)} %copy-done.3, ...), custom_call_target="tpu_custom_call" | custom-call | tf_op jit(solution)/shard_map/project_back/pallas_call | solution.py:1956
  536.4 1.3 copy-done.8
  537.7 0.7 maximum_maximum_fusion
  538.5 96.9 %weight_reduce.1 = (bf16[512,5120]{1,0:T(8,128)(2,1)}, f32[128,2048]{1,0:T(8,128)}) custom-call(bf16[2048,1280]{1,0:T(8,128)(2,1)} %get-tuple-element.57.grad_ref, bf16[512,2048]{1,0:T(8,128)(2,1)} %copy-done.8), custom_call_target="tpu_custom_call" | custom-call | tf_op jit(solution)/shard_map/weight_reduce/pallas_call | solution.py:1861
  635.4 8.1 %convert_element_type.79 = f32[512,5120]{1,0:T(8,128)} convert(bf16[512,5120]{1,0:T(8,128)(2,1)} %get-tuple-element.62) | non-fusion elementwise | flops 2621440 | bytes 15728640 | tf_op jit(solution)/shard_map/convert_element_type | solution.py:2087
  643.5 4.4 convert_element_type.80
  648.0 0.3 fusion
  648.3 0.9 add_convert_fusion
  649.2 1.3 fusion.4
  650.5 1.1 slice_reduce_fusion
  651.7 0.6 slice_bitcast_fusion.1
  652.3 0.5 slice_bitcast_fusion.3
  652.8 1.1 reduce-precision_convert_fusion.1
  654.0 8.6 %fusion.6 = f32[96,2048]{1,0:T(8,128)S(1)} fusion(bf16[4096,2048]{1,0:T(8,128)(2,1)} %get-tuple-element.64, bf16[32,4096]{1,0:T(8,128)(2,1)S(1)} %get-tuple-element.75, bf16[32,4096]{1,0:T(8,128)(2,1)S(1)} %get-tuple-element.76, bf16[32,4096]{1,0:T(8,128)(2,1)S(1)} %get-tuple-element.74), kind=kOutput, calls=%fused_computation.20 | convolution fusion | flops 1612972032 | bytes 18350080 | tf_op jit(solution)/shard_map/dot_general | solution.py:2099
  662.5 0.7 reduce_sum.109
  (58 shorter events, 0.4 us)
Async XLA Ops:
  7.2 137.8 %copy-start = (bf16[2048,32]{0,1:T(8,128)(2,1)S(1)}, bf16[2048,32]{0,1:T(8,128)(2,1)}, u32[]{:S(2)}) copy-start(bf16[2048,32]{0,1:T(8,128)(2,1)} %param.21) | copy-start | bytes 393220
  7.2 138.9 %all-gather.4.cloned.1.call-start = ((), (), s32[]{:S(2)}) async-start(), calls=%async_computation.1 | async-start | bytes 17301504 | tf_op jit(solution)/shard_map/all_gather | solution.py:1999
  9.5 1.0 copy-start.4
  10.5 2.5 copy-start.6
  87.9 2.4 copy-start.2
  90.2 1.5 copy-start.3
  93.7 49.0 %copy-start.5 = (bf16[128,2048]{1,0:T(8,128)(2,1)S(1)}, bf16[128,2048]{1,0:T(8,128)(2,1)}, u32[]{:S(2)}) copy-start(bf16[128,2048]{1,0:T(8,128)(2,1)} %x_ref.1) | copy-start | bytes 1572868
  120.3 1.6 copy-start.9
  121.9 22.1 %copy-start.19 = (f32[2048]{0:T(1024)S(1)}, f32[2048]{0:T(1024)}, u32[]{:S(2)}) copy-start(f32[2048]{0:T(1024)} %param.20) | copy-start | bytes 24580
  121.9 23.4 %copy-start.21 = (s32[128,8]{0,1:T(8,128)S(1)}, s32[128,8]{0,1:T(8,128)}, u32[]{:S(2)}) copy-start(s32[128,8]{0,1:T(8,128)} %param.14) | copy-start | bytes 12292
  143.0 1.0 copy-start.11
  144.1 0.8 copy-start.13
  267.6 95.3 %all-to-all-start = ((f32[32,1,128]{2,1,0:T(1,128)}), f32[32,1,128]{2,1,0:T(1,128)S(1)}, u32[]{:S(2)}, u32[]{:S(2)}) async-start(f32[32,1,128]{2,1,0:T(1,128)} %bitcast.73), calls=%async_computation | async-start | bytes 32768 | tf_op jit(solution)/shard_map/all_to_all | solution.py:2029
  272.4 378.1 %all-gather.6.cloned.1.call-start = ((), (), s32[]{:S(2)}) async-start(), calls=%async_computation.2 | async-start | bytes 1351680 | tf_op jit(solution)/shard_map/all_gather | solution.py:2085
  362.9 23.0 %copy-start.14 = (bf16[1024,2048]{1,0:T(8,128)(2,1)S(1)}, bf16[1024,2048]{1,0:T(8,128)(2,1)}, u32[]{:S(2)}) copy-start(bf16[1024,2048]{1,0:T(8,128)(2,1)} %w_out_ref.1) | copy-start | bytes 12582916
  385.9 3.4 copy-start.22
  513.4 1.6 copy-start.7
  515.0 1.3 copy-start.10
  536.4 1.3 copy-start.8
  635.4 8.1 %copy-start.15 = (bf16[1024,2048]{1,0:T(8,128)(2,1)S(1)}, bf16[1024,2048]{1,0:T(8,128)(2,1)}, u32[]{:S(2)}) copy-start(bf16[1024,2048]{1,0:T(8,128)(2,1)} %get-tuple-element.63) | copy-start | bytes 12582916
  643.5 4.5 copy-start.17
  643.5 4.5 copy-start.20
  643.5 4.8 copy-start.12
  643.5 4.8 copy-start.18
  648.0 1.3 copy-start.16
  653.9 9.4 %copy-start.1 = (bf16[2048,32]{0,1:T(8,128)(2,1)S(1)}, bf16[2048,32]{0,1:T(8,128)(2,1)}, u32[]{:S(2)}) copy-start(bf16[2048,32]{0,1:T(8,128)(2,1)} %param.21) | copy-start | bytes 393220
Sparse Core Ops, SparseCore 0:
  10.9 135.1 all-gather.3
  538.6 75.2 all-gather.5

commit v2 on v1

--- a/solution.py
+++ b/solution.py
@@ -1825,12 +1825,8 @@
     single = HEAD_SIZE
     heads = QUERY_HEADS // 4 * HEAD_SIZE
     writes = []
-
-    @pl.loop(0, LADDER)
-    def _(n):
-        closed(n)
-
     for n in range(4):
+        pl.loop(n * PER, (n + 1) * PER)(closed)
         who = near[n][1]
         for c, (base, width, offset) in enumerate(
             (

time: 671 us -> 671 us (level)
  no operation moved by 1% of the time
where the time goes in v2:
time: 671 us; the launch traced here: 670 us
  Pallas kernels  587 us (87%)
  other arithmetic  24.8 us (4%)
  matrix products  19.2 us (3%)
  local copies, waits for them, and re-layouts  18.5 us (3%)
  between operations  14.4 us (2%)
    pallas_call x2, Pallas kernels, reduce_all(): pl.pallas_call(functools.partial(reduce_kernel, weight is not None), out_...  209 us
    pallas_call x1, Pallas kernels, run_experts(): pl.pallas_call(experts_kernel, out_shape=[jax.ShapeDtypeStruct((total, wi...  121 us
    pallas_call x1, Pallas kernels, weight_reduce(): pl.pallas_call(weight_kernel, out_shape=[jax.ShapeDtypeStruct((depth, col...  96.8 us
    pallas_call x1, Pallas kernels, start_exchange(): pl.pallas_call(start_kernel, out_shape=[jax.ShapeDtypeStruct((tok * 4, wi...  74.9 us
    pallas_call x1, Pallas kernels, attend(): pl.pallas_call(attend_kernel, out_shape=[out((seq, width), bf), out((seq,...  26.6 us
    pallas_call x1, Pallas kernels, fold_sequence(): pl.pallas_call(fold_kernel, out_shape=jax.ShapeDtypeStruct((tok, width),...  20.9 us
    pallas_call x1, Pallas kernels, project_back(): pl.pallas_call(project_back_kernel, out_shape=[jax.ShapeDtypeStruct((seq,...  20.1 us
    pallas_call x1, Pallas kernels, spread_sequence(): pl.pallas_call(spread_kernel, out_shape=jax.ShapeDtypeStruct((tok * 4, wi...  17.7 us
  transfers between devices with their start and end apart: 3, of which 0 were waited for; matrix products, arithmetic and copies ran while one was open for 3% of the time, Pallas kernels for 46%

profile of v2, /device:TPU:0, one launch (start us, length us, event | category | flops | bytes accessed | tf_op | source)
XLA Modules:
  0.0 670.0 jit_solution(6622833380801812529)
XLA Ops:
  7.2 0.7 all-gather.4.cloned.1.call-update
  7.9 1.5 copy.35.seg_col.refs_12_
  9.5 1.0 copy-done.4
  10.5 2.5 copy-done.6
  13.0 74.9 %start_exchange.1 = (bf16[512,2048]{1,0:T(8,128)(2,1)S(1)}, bf16[2048,1280]{1,0:T(8,128)(2,1)S(1)}) custom-call(bf16[128,2048]{1,0:T(8,128)(2,1)S(1)} %copy-done.4, bf16[512,5120]{1,0:T(8,128)(2,1)S(1)} %copy-done.6), custom_call_target="tpu_custom_call" | custom-call | tf_op jit(solution)/shard_map/start_exchange/pallas_call | solution.py:1601
  87.9 2.3 copy-done.2
  90.2 1.5 copy-done.3
  91.7 1.0 multiply_sine_fusion
  92.7 1.0 pad_maximum_fusion
  93.7 26.6 %attend.1 = (bf16[512,2048]{1,0:T(8,128)(2,1)}, f32[512,1280]{1,0:T(8,128)}, bf16[512,1024]{1,0:T(8,128)(2,1)}, bf16[512,128]{1,0:T(8,128)(2,1)}, bf16[512,128]{...) custom-call(bf16[512,2048]{1,0:T(8,128)(2,1)} %copy-done.3, ...), custom_call_target="tpu_custom_call" | custom-call | tf_op jit(solution)/shard_map/attend/pallas_call | solution.py:881
  120.3 1.6 copy-done.9
  121.9 20.9 %fold_sequence.1 = f32[128,2048]{1,0:T(8,128)S(1)} custom-call(bf16[512,2048]{1,0:T(8,128)(2,1)S(1)} %copy-done.9), custom_call_target="tpu_custom_call" | custom-call | tf_op jit(solution)/shard_map/fold_sequence/pallas_call | solution.py:1720
  142.8 0.2 multiply_reduce_fusion.2
  143.0 1.0 copy-done.11
  144.0 0.2 multiply_convert_fusion.x_ref
  144.1 0.8 copy-done.13
  144.9 0.3 fusion.25
  145.3 0.1 convolution_select_fusion
  145.5 0.6 pad_maximum_fusion.1.table_ref
  146.1 121.4 %run_experts.1 = (bf16[4096,2048]{1,0:T(8,128)(2,1)}, f32[2048,128]{1,0:T(8,128)}, bf16[4096,2048]{1,0:T(8,128)(2,1)}, bf16[4096,2048]{1,0:T(8,128)(2,1)}, f32[3...) custom-call(bf16[128,2048]{1,0:T(8,128)(2,1)} %copy-done.13, ...), custom_call_target="tpu_custom_call" | custom-call | tf_op jit(solution)/shard_map/run_experts/pallas_call | solution.py:731
  267.6 4.8 all-to-all-start
  272.4 0.0 all-gather.6.cloned.1.call-start
  272.5 0.1 pad.5.clone
  272.5 90.3 %reduce_all.2 = (bf16[128,2048]{1,0:T(8,128)(2,1)}, f32[1,3,2048,768]{3,2,1,0:T(8,128)}) custom-call(bf16[4096,2048]{1,0:T(8,128)(2,1)} %get-tuple-element.43.refs_0_, bf16[2,2048,2048]{2,1,0:T(8,128)(2,1)} %get-tuple-element.44.refs_1_, bf16[3,2048,768]{2,1,0:T(8,128)(2,1)} %get-tuple-element.45.refs_2_), custom_call_target="tpu_custom_call" | custom-call | tf_op jit(solution)/shard_map/reduce_all/pallas_call | solution.py:1479
  362.9 2.4 multiply_reduce_fusion
  365.4 2.8 fusion.24
  368.2 17.7 %spread_sequence.1 = bf16[512,2048]{1,0:T(8,128)(2,1)S(1)} custom-call(bf16[128,2048]{1,0:T(8,128)(2,1)S(1)} %get-tuple-element.70.x_ref), custom_call_target="tpu_custom_call" | custom-call | tf_op jit(solution)/shard_map/spread_sequence/pallas_call | solution.py:1665
  385.9 3.4 convolution_convert_fusion.1.refs_6_
  389.2 4.4 convolution_convert_fusion.refs_1_
  393.6 119.0 %reduce_all.3 = (bf16[128,2048]{1,0:T(8,128)(2,1)}, bf16[1024,2048]{1,0:T(8,128)(2,1)}, bf16[512,1280]{1,0:T(8,128)(2,1)}, f32[8,128]{1,0:T(8,128)}) custom-call(bf16[4096,2048]{1,0:T(8,128)(2,1)} %get-tuple-element.41.refs_0_, bf16[1024,2048]{1,0:T(8,128)(2,1)} %convolution_convert_fusion.refs_1_, bf16[512,1024]{1,0:T(8,128)(2,1)} %get-tuple-element.48.refs_2_, ...), custom_call_target="tpu_custom_call" | custom-call | tf_op jit(solution)/shard_map/reduce_all/pallas_call | solution.py:1479
  512.6 0.8 slice_bitcast_fusion.6
  513.4 1.6 copy-done.7
  515.0 1.3 copy-done.10
  516.3 20.1 %project_back.1 = (bf16[512,2048]{1,0:T(8,128)(2,1)S(1)}, bf16[2048,1280]{1,0:T(8,128)(2,1)}, f32[1,2048]{1,0:T(1,128)S(1)}, f32[1,3,2048,768]{3,2,1,0:T(8,128)}) custom-call(bf16[512,1280]{1,0:T(8,128)(2,1)S(1)} %copy-done.10, bf16[2048,1280]{1,0:T(8,128)(2,1)} %copy-done.2, bf16[512,2048]{1,0:T(8,128)(2,1)S(1)} %copy-done.7, bf16[512,2048]{1,0:T(8,128)(2,1)} %copy-done.3, ...), custom_call_target="tpu_custom_call" | custom-call | tf_op jit(solution)/shard_map/project_back/pallas_call | solution.py:1952
  536.4 1.3 copy-done.8
  537.7 0.7 maximum_maximum_fusion
  538.5 96.8 %weight_reduce.1 = (bf16[512,5120]{1,0:T(8,128)(2,1)}, f32[128,2048]{1,0:T(8,128)}) custom-call(bf16[2048,1280]{1,0:T(8,128)(2,1)} %get-tuple-element.57.grad_ref, bf16[512,2048]{1,0:T(8,128)(2,1)} %copy-done.8), custom_call_target="tpu_custom_call" | custom-call | tf_op jit(solution)/shard_map/weight_reduce/pallas_call | solution.py:1857
  635.3 8.1 %convert_element_type.79 = f32[512,5120]{1,0:T(8,128)} convert(bf16[512,5120]{1,0:T(8,128)(2,1)} %get-tuple-element.62) | non-fusion elementwise | flops 2621440 | bytes 15728640 | tf_op jit(solution)/shard_map/convert_element_type | solution.py:2083
  643.4 4.4 convert_element_type.80
  647.8 0.3 fusion
  648.2 0.9 add_convert_fusion
  649.1 1.3 fusion.4
  650.4 1.1 slice_reduce_fusion
  651.5 0.6 slice_bitcast_fusion.1
  652.1 0.5 slice_bitcast_fusion.3
  652.6 1.1 reduce-precision_convert_fusion.1
  653.8 8.6 %fusion.6 = f32[96,2048]{1,0:T(8,128)S(1)} fusion(bf16[4096,2048]{1,0:T(8,128)(2,1)} %get-tuple-element.64, bf16[32,4096]{1,0:T(8,128)(2,1)S(1)} %get-tuple-element.75, bf16[32,4096]{1,0:T(8,128)(2,1)S(1)} %get-tuple-element.76, bf16[32,4096]{1,0:T(8,128)(2,1)S(1)} %get-tuple-element.74), kind=kOutput, calls=%fused_computation.20 | convolution fusion | flops 1612972032 | bytes 18350080 | tf_op jit(solution)/shard_map/dot_general | solution.py:2095
  662.4 0.7 reduce_sum.109
  (58 shorter events, 0.4 us)
Async XLA Ops:
  7.2 137.8 %copy-start = (bf16[2048,32]{0,1:T(8,128)(2,1)S(1)}, bf16[2048,32]{0,1:T(8,128)(2,1)}, u32[]{:S(2)}) copy-start(bf16[2048,32]{0,1:T(8,128)(2,1)} %param.21) | copy-start | bytes 393220
  7.2 138.9 %all-gather.4.cloned.1.call-start = ((), (), s32[]{:S(2)}) async-start(), calls=%async_computation.1 | async-start | bytes 17301504 | tf_op jit(solution)/shard_map/all_gather | solution.py:1995
  9.5 1.0 copy-start.4
  10.5 2.5 copy-start.6
  87.9 2.4 copy-start.2
  90.2 1.5 copy-start.3
  93.7 49.0 %copy-start.5 = (bf16[128,2048]{1,0:T(8,128)(2,1)S(1)}, bf16[128,2048]{1,0:T(8,128)(2,1)}, u32[]{:S(2)}) copy-start(bf16[128,2048]{1,0:T(8,128)(2,1)} %x_ref.1) | copy-start | bytes 1572868
  120.3 1.6 copy-start.9
  121.9 22.1 %copy-start.19 = (f32[2048]{0:T(1024)S(1)}, f32[2048]{0:T(1024)}, u32[]{:S(2)}) copy-start(f32[2048]{0:T(1024)} %param.20) | copy-start | bytes 24580
  121.9 23.4 %copy-start.21 = (s32[128,8]{0,1:T(8,128)S(1)}, s32[128,8]{0,1:T(8,128)}, u32[]{:S(2)}) copy-start(s32[128,8]{0,1:T(8,128)} %param.14) | copy-start | bytes 12292
  143.0 1.0 copy-start.11
  144.1 0.8 copy-start.13
  267.6 95.3 %all-to-all-start = ((f32[32,1,128]{2,1,0:T(1,128)}), f32[32,1,128]{2,1,0:T(1,128)S(1)}, u32[]{:S(2)}, u32[]{:S(2)}) async-start(f32[32,1,128]{2,1,0:T(1,128)} %bitcast.73), calls=%async_computation | async-start | bytes 32768 | tf_op jit(solution)/shard_map/all_to_all | solution.py:2025
  272.4 377.9 %all-gather.6.cloned.1.call-start = ((), (), s32[]{:S(2)}) async-start(), calls=%async_computation.2 | async-start | bytes 1351680 | tf_op jit(solution)/shard_map/all_gather | solution.py:2081
  362.9 23.0 %copy-start.14 = (bf16[1024,2048]{1,0:T(8,128)(2,1)S(1)}, bf16[1024,2048]{1,0:T(8,128)(2,1)}, u32[]{:S(2)}) copy-start(bf16[1024,2048]{1,0:T(8,128)(2,1)} %w_out_ref.1) | copy-start | bytes 12582916
  385.9 3.4 copy-start.22
  513.4 1.6 copy-start.7
  515.0 1.3 copy-start.10
  536.4 1.3 copy-start.8
  635.2 8.1 %copy-start.15 = (bf16[1024,2048]{1,0:T(8,128)(2,1)S(1)}, bf16[1024,2048]{1,0:T(8,128)(2,1)}, u32[]{:S(2)}) copy-start(bf16[1024,2048]{1,0:T(8,128)(2,1)} %get-tuple-element.63) | copy-start | bytes 12582916
  643.3 4.5 copy-start.17
  643.3 4.5 copy-start.20
  643.3 4.8 copy-start.12
  643.3 4.8 copy-start.18
  647.8 1.3 copy-start.16
  653.8 9.3 %copy-start.1 = (bf16[2048,32]{0,1:T(8,128)(2,1)S(1)}, bf16[2048,32]{0,1:T(8,128)(2,1)}, u32[]{:S(2)}) copy-start(bf16[2048,32]{0,1:T(8,128)(2,1)} %param.21) | copy-start | bytes 393220
Sparse Core Ops, SparseCore 0:
  10.9 135.1 all-gather.3
  538.6 75.2 all-gather.5
